TPU v7x, 512 devices: a 4x2x32 block of a 4x8x32 slice. The times are simulated.
512 devices in a mesh: groups: 2 (over y), row: 32 (over z), col: 4 (over x), rep: 2 (over core).
Axes of the slice: x: 4, y: 2, z: 32, core: 2. Of those that a mesh axis runs over, the one named last changes fastest.
The devices are a block of a 4x8x32 slice.
Arguments:
- kernel: float32 [32768, 16384], P(('groups', 'row'), ('col', 'rep')), parts along dimension 0, may hold values from 0 to 2, as said below
- source: float32 [64, 16384], P('groups', 'row'), parts along dimension 0, may hold values from 0.5 to 2, as said below
- target: float32 [64, 16384], P('groups', ('col', 'rep')), parts along dimension 0, may hold values from 0.5 to 2, as said below
Outputs:
- left_scale: float32 [64, 16384], P('groups', 'row'), parts along dimension 0
- right_scale: float32 [64, 16384], P('groups', ('col', 'rep')), parts along dimension 0
- errors: float32 [6, 32], P('groups'), parts along dimension 0
There are 2 independent parts, one for each index of `groups`. A program takes and returns all parts, laid end to end along the dimension named above; each array names one. Nothing has to cross between parts.
Inputs may be any that keep to these rules, and one draw needn't show every extreme that they name: `kernel`: every entry is positive. `source`: every entry is positive. `target`: every entry is positive.
All inputs are finite; a program needn't handle non-finite values.
Results may differ from a plain program's by a relative error of at most 0.0001.
Values sent between devices are 32-bit elements; how exact they have to be, the bound alone decides.
No kernel may reach another device: no remote copies, remote signals or barrier semaphores. Data moves between devices by JAX's collectives and lax.ppermute only.
A program may use at most 64 MiB of HBM per device.

v0:
```python
import jax
import jax.numpy as jnp
from jax import lax
from jax.sharding import PartitionSpec as P

N = 16384
ITERS = 3


def from_everyone(array, axis):
    copies = jnp.broadcast_to(array, (lax.axis_size(axis), *array.shape))
    return lax.all_to_all(copies, axis, split_axis=0, concat_axis=0, tiled=True)


def over_copies(array, axis):
    everything = from_everyone(array, axis)
    return jnp.sum(everything, axis=0)


def in_blocks(array, dim, length):
    shape = array.shape
    pieces = array.reshape(*shape[:dim], length, shape[dim] // length, *shape[dim + 1 :])
    return jnp.moveaxis(pieces, dim, 0)


def sent_and_summed(array, axis, dim):
    pieces = in_blocks(array, dim, lax.axis_size(axis))
    arrived = lax.all_to_all(pieces, axis, split_axis=0, concat_axis=0, tiled=True)
    return arrived.sum(axis=0)


def laid_out(pieces, dim):
    pieces = jnp.moveaxis(pieces, 0, dim)
    shape = pieces.shape
    return pieces.reshape(*shape[:dim], shape[dim] * shape[dim + 1], *shape[dim + 2 :])


def collect(array, axis, dim):
    pieces = from_everyone(array, axis)
    return laid_out(pieces, dim)


def by_axis(array, axes):
    for axis in axes:
        array = lax.psum(array, axis)
    return array


def local(kernel, source, target):
    columns = kernel.shape[1]
    right_scale = jnp.ones(target.shape, jnp.float32)
    left_scale = source
    share = columns // lax.axis_size("row")
    offset = lax.axis_index("row") * share
    terms = []
    for step in range(ITERS):
        partial_value = lax.dot_general(
            right_scale, kernel, (((1,), (1,)), ((), ())), precision=lax.Precision.HIGHEST
        )
        left_scale = source / over_copies(partial_value, ("col", "rep"))
        back = jnp.dot(left_scale, kernel, precision=lax.Precision.HIGHEST)
        old_piece = lax.dynamic_slice_in_dim(right_scale, offset, share, 1)
        target_piece = lax.dynamic_slice_in_dim(target, offset, share, 1)
        total_piece = sent_and_summed(back, "row", 1)
        right_scale = collect(target_piece / total_piece, "row", 1)
        term = jnp.sum(jnp.abs(old_piece * total_piece - target_piece), axis=1) / N
        terms.append(term)
    stacked = by_axis(jnp.stack(terms), ("row", "col", "rep"))
    return (left_scale, right_scale, stacked)


def solution(mesh):
    return jax.shard_map(
        local,
        mesh=mesh,
        in_specs=(
            P(("groups", "row"), ("col", "rep")),
            P("groups", "row"),
            P("groups", ("col", "rep")),
        ),
        out_specs=(P("groups", "row"), P("groups", ("col", "rep")), P("groups", None)),
        check_vma=False,
    )
```

profile of v0, /device:TPU:33, one launch (start us, length us, event | category | flops | bytes accessed | tf_op | source)
XLA Modules:
  0.0 451.9 jit_solution(4674217970748007036)
XLA Ops:
  0.6 6.0 %fusion = f32[32,512]{1,0:T(8,128)S(1)} fusion(f32[512,2048]{1,0:T(8,128)} %param.3), kind=kOutput, calls=%fused_computation.3 | convolution fusion | flops 402653184 | bytes 4259840 | tf_op jit(solution)/shard_map/dot_general | solution.py:57
  6.8 53.2 %all_to_all.45 = f32[8,32,512]{2,1,0:T(8,128)S(1)} all-to-all(f32[8,32,512]{2,1,0:T(8,128)S(1)} %broadcast_in_dim.22), channel_id=1, replica_groups=mesh['groups'=2,'row'=32,'col'=4,'rep'=2] {'col','rep'}, dimensions={0} | all-to-all | bytes 1048576 | tf_op jit(solution)/shard_map/all_to_all | solution.py:12
  60.0 4.7 %fusion.4 = f32[32,2048]{1,0:T(8,128)S(1)} fusion(f32[512,2048]{1,0:T(8,128)} %param.3, f32[32,512]{1,0:T(8,128)S(1)} %copy-done, f32[32,512]{1,0:T(8,128)S(1)} %reduce_sum.81), kind=kOutput, calls=%fused_computation.7 | convolution fusion | flops 402669568 | bytes 4587520 | tf_op jit(solution)/shard_map/dot_general | solution.py:61
  65.3 1.0 reshape.57
  66.3 7.4 %all-to-all-start.1 = ((f32[32,1,2048]{2,1,0:T(1,128)}), f32[32,1,2048]{2,1,0:T(1,128)S(1)}, u32[]{:S(2)}, u32[]{:S(2)}) async-start(f32[32,1,2048]{2,1,0:T(1,128)} %reshape.57), calls=%async_computation.1 | async-start | bytes 524288 | tf_op jit(solution)/shard_map/all_to_all | solution.py:28
  73.7 40.0 %all-to-all-done.1 = f32[32,1,2048]{2,1,0:T(1,128)S(1)} async-done(((f32[32,1,2048]{2,1,0:T(1,128)}), f32[32,1,2048]{2,1,0:T(1,128)S(1)}, u32[]{:S(2)}, u32[]{:S(2)}) %all-to-all-start.1) | async-done | bytes 262176 | tf_op jit(solution)/shard_map/all_to_all | solution.py:28
  113.7 0.6 broadcast.35
  114.3 1.3 reduce
  115.9 0.8 dynamic-slice_divide_fusion.2
  117.1 42.2 %all_to_all.46 = f32[32,1,2048]{2,1,0:T(1,128)S(1)} all-to-all(f32[32,1,2048]{2,1,0:T(1,128)S(1)} %reshape.59), channel_id=1, replica_groups=mesh['groups'=2,'row'=32,'col'=4,'rep'=2] {'row'}, dimensions={0} | all-to-all | bytes 524288 | tf_op jit(solution)/shard_map/all_to_all | solution.py:12
  159.2 1.3 reduce.1
  161.3 6.0 %fusion.7 = f32[32,512]{1,0:T(8,128)S(1)} fusion(f32[32,2048]{1,0:T(8,128)S(1)} %reshape.52, f32[512,2048]{1,0:T(8,128)} %param.3), kind=kOutput, calls=%fused_computation.20 | convolution fusion | flops 402653184 | bytes 4521984 | tf_op jit(solution)/shard_map/dot_general | solution.py:57
  167.3 17.1 %all_to_all.47 = f32[8,32,512]{2,1,0:T(8,128)S(1)} all-to-all(f32[8,32,512]{2,1,0:T(8,128)S(1)} %broadcast_in_dim.24), channel_id=1, replica_groups=mesh['groups'=2,'row'=32,'col'=4,'rep'=2] {'col','rep'}, dimensions={0} | all-to-all | bytes 1048576 | tf_op jit(solution)/shard_map/all_to_all | solution.py:12
  184.5 4.7 %fusion.2 = f32[32,2048]{1,0:T(8,128)S(1)} fusion(f32[512,2048]{1,0:T(8,128)} %param.3, f32[32,512]{1,0:T(8,128)S(1)} %copy-done, f32[32,512]{1,0:T(8,128)S(1)} %reduce_sum.83), kind=kOutput, calls=%fused_computation.5 | convolution fusion | flops 402669568 | bytes 4587520 | tf_op jit(solution)/shard_map/dot_general | solution.py:61
  190.0 43.4 %all_to_all.48 = f32[32,1,2048]{2,1,0:T(1,128)S(1)} all-to-all(f32[32,1,2048]{2,1,0:T(1,128)S(1)} %reshape.61), channel_id=1, replica_groups=mesh['groups'=2,'row'=32,'col'=4,'rep'=2] {'row'}, dimensions={0} | all-to-all | bytes 524288 | tf_op jit(solution)/shard_map/all_to_all | solution.py:28
  233.4 1.3 reduce.2
  235.0 0.8 dynamic-slice_divide_fusion.1
  236.2 42.6 %all_to_all.49 = f32[32,1,2048]{2,1,0:T(1,128)S(1)} all-to-all(f32[32,1,2048]{2,1,0:T(1,128)S(1)} %reshape.63), channel_id=1, replica_groups=mesh['groups'=2,'row'=32,'col'=4,'rep'=2] {'row'}, dimensions={0} | all-to-all | bytes 524288 | tf_op jit(solution)/shard_map/all_to_all | solution.py:12
  278.8 1.3 reduce.3
  280.9 6.0 %fusion.8 = f32[32,512]{1,0:T(8,128)S(1)} fusion(f32[32,2048]{1,0:T(8,128)S(1)} %reshape.54, f32[512,2048]{1,0:T(8,128)} %param.3), kind=kOutput, calls=%fused_computation.21 | convolution fusion | flops 402653184 | bytes 4521984 | tf_op jit(solution)/shard_map/dot_general | solution.py:57
  286.9 17.1 %all_to_all.50 = f32[8,32,512]{2,1,0:T(8,128)S(1)} all-to-all(f32[8,32,512]{2,1,0:T(8,128)S(1)} %broadcast_in_dim.26), channel_id=1, replica_groups=mesh['groups'=2,'row'=32,'col'=4,'rep'=2] {'col','rep'}, dimensions={0} | all-to-all | bytes 1048576 | tf_op jit(solution)/shard_map/all_to_all | solution.py:12
  304.2 4.7 %fusion.9 = f32[32,2048]{1,0:T(8,128)S(1)} fusion(f32[32,512]{1,0:T(8,128)S(1)} %div.37, f32[512,2048]{1,0:T(8,128)} %param.3), kind=kOutput, calls=%fused_computation.22 | convolution fusion | flops 402653184 | bytes 4521984 | tf_op jit(solution)/shard_map/dot_general | solution.py:61
  309.7 43.4 %all_to_all.51 = f32[32,1,2048]{2,1,0:T(1,128)S(1)} all-to-all(f32[32,1,2048]{2,1,0:T(1,128)S(1)} %reshape.65), channel_id=1, replica_groups=mesh['groups'=2,'row'=32,'col'=4,'rep'=2] {'row'}, dimensions={0} | all-to-all | bytes 524288 | tf_op jit(solution)/shard_map/all_to_all | solution.py:28
  353.1 1.3 reduce.4
  354.7 1.0 abs_reduce_fusion.2
  355.7 1.0 reshape.67
  356.7 5.2 %all-to-all-start.8 = ((f32[32,1,2048]{2,1,0:T(1,128)}), f32[32,1,2048]{2,1,0:T(1,128)S(1)}, u32[]{:S(2)}, u32[]{:S(2)}) async-start(f32[32,1,2048]{2,1,0:T(1,128)} %reshape.67), calls=%async_computation.8 | async-start | bytes 524288 | tf_op jit(solution)/shard_map/all_to_all | solution.py:12
  362.0 61.2 %psum.21 = f32[3,32]{1,0:T(4,128)S(1)} all-reduce(f32[3,32]{1,0:T(4,128)S(1)} %pad_maximum_fusion), channel_id=1, replica_groups=mesh['groups'=2,'row'=32,'col'=4,'rep'=2] {'row'}, use_global_device_ids=true, to_apply=%region_9.0 | all-reduce | flops 96 | bytes 768 | tf_op jit(solution)/shard_map/psum | solution.py:45
  423.2 6.9 %psum.22 = f32[3,32]{1,0:T(4,128)S(1)} all-reduce(f32[3,32]{1,0:T(4,128)S(1)} %psum.21), channel_id=1, replica_groups=mesh['groups'=2,'row'=32,'col'=4,'rep'=2] {'col'}, use_global_device_ids=true, to_apply=%region_10.0 | all-reduce | flops 96 | bytes 768 | tf_op jit(solution)/shard_map/psum | solution.py:45
  430.1 19.1 %psum.23 = f32[3,32]{1,0:T(4,128)} all-reduce(f32[3,32]{1,0:T(4,128)S(1)} %psum.22), channel_id=1, replica_groups=mesh['groups'=2,'row'=32,'col'=4,'rep'=2] {'rep'}, use_global_device_ids=true, to_apply=%region_11.0 | all-reduce | flops 96 | bytes 768 | tf_op jit(solution)/shard_map/psum | solution.py:45
  449.2 1.3 reduce.5
  451.0 0.9 reshape.56
  (42 shorter events, 6.1 us)
Async XLA Ops:
  0.6 59.4 %copy-start = (f32[32,512]{1,0:T(8,128)S(1)}, f32[32,512]{1,0:T(8,128)}, u32[]{:S(2)}) copy-start(f32[32,512]{1,0:T(8,128)} %param.4) | copy-start | bytes 196612
  66.3 47.4 %all-to-all-start.1 = ((f32[32,1,2048]{2,1,0:T(1,128)}), f32[32,1,2048]{2,1,0:T(1,128)S(1)}, u32[]{:S(2)}, u32[]{:S(2)}) async-start(f32[32,1,2048]{2,1,0:T(1,128)} %reshape.57), calls=%async_computation.1 | async-start | bytes 524288 | tf_op jit(solution)/shard_map/all_to_all | solution.py:28
  304.1 50.5 %copy-start.1 = (f32[32,512]{1,0:T(8,128)}, f32[32,512]{1,0:T(8,128)S(1)}, u32[]{:S(2)}) copy-start(f32[32,512]{1,0:T(8,128)S(1)} %div.37) | copy-start | bytes 196612
  356.7 92.4 %all-to-all-start.8 = ((f32[32,1,2048]{2,1,0:T(1,128)}), f32[32,1,2048]{2,1,0:T(1,128)S(1)}, u32[]{:S(2)}, u32[]{:S(2)}) async-start(f32[32,1,2048]{2,1,0:T(1,128)} %reshape.67), calls=%async_computation.8 | async-start | bytes 524288 | tf_op jit(solution)/shard_map/all_to_all | solution.py:12
where the time goes:
time: 453 us; the launch traced here: 452 us
  blocking collectives  346 us (76%)
  waiting for transfers between devices  40 us (9%)
  matrix products  32.1 us (7%)
  starting transfers between devices  12.5 us (3%)
  other arithmetic  10.7 us (2%)
  local copies, waits for them, and re-layouts  9.31 us (2%)
    all_to_all x5, blocking collectives, from_everyone(): return lax.all_to_all(copies, axis, split_axis=0, concat_axis=0, tiled=True)  172 us
    psum x3, blocking collectives, by_axis(): array = lax.psum(array, axis)  87.2 us
    all_to_all x2, blocking collectives, sent_and_summed(): lax.all_to_all(pieces, axis, split_axis=0, concat_axis=0, tiled=True)  86.8 us
    all_to_all x1, waiting for transfers between devices, sent_and_summed(): lax.all_to_all(pieces, axis, split_axis=0, concat_axis=0, tiled=True)  40 us
    dot_general x3, matrix products, local(): lax.dot_general(right_scale, kernel, (((1,), (1,)), ((), ())), precision=...  18.1 us
    dot_general x3, matrix products, local(): back = jnp.dot(left_scale, kernel, precision=lax.Precision.HIGHEST)  14 us
  transfers between devices with their start and end apart: 2, of which 1 were waited for; matrix products, arithmetic and copies ran while one was open for 0% of the time, Pallas kernels for 0%

commit v1 on v0

v1 whole, which is shorter than its diff:
```python
import jax
import jax.numpy as jnp
from jax import lax
from jax.sharding import Mesh, PartitionSpec as P

ITERS = 3
NEAR = 4


def exchange(pieces, axis):
    return lax.all_to_all(pieces, axis, split_axis=0, concat_axis=0, tiled=True)


def from_everyone(array, axis, size):
    return exchange(jnp.broadcast_to(array, (size, *array.shape)), axis)


def solution(mesh):
    shape = mesh.shape
    far = shape["row"] // NEAR
    names = ("groups", "far", "near", "col", "rep")
    split = Mesh(
        mesh.devices.reshape(shape["groups"], far, NEAR, shape["col"], shape["rep"]), names
    )
    block = ("col", "rep")
    blocks = shape["col"] * shape["rep"]

    def total_over_rows(back):
        pairs, columns = back.shape
        few, share = pairs // NEAR, columns // far
        near = exchange(back.reshape(NEAR, few, columns), "near").sum(axis=0)
        pieces = near.reshape(few, far, share).transpose(1, 0, 2)
        piece = exchange(pieces, "far").sum(axis=0)
        mine = from_everyone(piece, "far", far)
        everything = from_everyone(mine, "near", NEAR)
        return everything.transpose(0, 2, 1, 3).reshape(pairs, columns)

    def local(kernel, source, target):
        count = blocks * target.shape[1]
        right_scale = jnp.ones(target.shape, jnp.float32)
        terms = []
        for step in range(ITERS):
            if step == 0:
                partial_value = jnp.sum(kernel, axis=1).reshape(-1, 128)
                value = from_everyone(partial_value, block, blocks).sum(axis=0).reshape(1, -1)
            else:
                partial_value = lax.dot_general(
                    right_scale, kernel, (((1,), (1,)), ((), ())), precision=lax.Precision.HIGH
                )
                value = from_everyone(partial_value, block, blocks).sum(axis=0)
            left_scale = source / value
            back = jnp.dot(left_scale, kernel, precision=lax.Precision.HIGH)
            total = total_over_rows(back)
            terms.append(jnp.sum(jnp.abs(right_scale * total - target), axis=1))
            right_scale = target / total
        errors = from_everyone(jnp.stack(terms), block, blocks).sum(axis=0) / count
        return left_scale, right_scale, errors

    return jax.shard_map(
        local,
        mesh=split,
        in_specs=(
            P(("groups", "far", "near"), block),
            P("groups", ("far", "near")),
            P("groups", block),
        ),
        out_specs=(P("groups", ("far", "near")), P("groups", block), P("groups", None)),
        check_vma=False,
    )
```

time: 453 us -> 335 us (0.74)
  waiting for transfers between devices: 40 us -> 0 us
  blocking collectives: 346 us -> 310 us
  matrix products: 32.1 us -> 18.8 us
  starting transfers between devices: 12.5 us -> 0 us
  local copies, waits for them, and re-layouts: 9.31 us -> 0.2 us
  other arithmetic: 10.7 us -> 4.34 us
    psum x3 -> x0, blocking collectives: 87.2 us -> none  [by_axis(): array = lax.psum(array, axis)]
    all_to_all x7 -> x16, blocking collectives: 259 us -> 310 us  [exchange(): return lax.all_to_all(pieces, axis, split_axis=0, concat_axis=0, tiled=True)]
    all_to_all x2 -> x0, waiting for transfers between devices: 40 us -> none  [the longest x1 40 us: sent_and_summed(): lax.all_to_all(pieces, axis, split_axis=0, concat_axis=0, tiled=True)]
    all_to_all x2 -> x0, starting transfers between devices: 12.5 us -> none  [the longest x1 7.37 us: sent_and_summed(): lax.all_to_all(pieces, axis, split_axis=0, concat_axis=0, tiled=True)]
    dot_general x3 -> x2, matrix products: 18.1 us -> 8.2 us  [local(): lax.dot_general(right_scale, kernel, (((1,), (1,)), ((), ())), precision=...]
    all_to_all x6 -> x0, other arithmetic: 7.81 us -> none  [the longest x3 3.9 us: from_everyone(): return lax.all_to_all(copies, axis, split_axis=0, concat_axis=0, tiled=True)]
    unnamed x16 -> x6, local copies, waits for them, and re-layouts: 4.64 us -> 0.01 us
  transfers between devices with their start and end apart: 2 -> 0, of which waited for: 1 -> 0; matrix products, arithmetic and copies ran while one was open for 0% -> 0% of each run, Pallas kernels for 0% -> 0%
where the time goes in v1:
time: 335 us; the launch traced here: 334 us
  blocking collectives  310 us (93%)
  matrix products  18.8 us (6%)
  other arithmetic  4.34 us (1%)
    all_to_all x16, blocking collectives, exchange(): return lax.all_to_all(pieces, axis, split_axis=0, concat_axis=0, tiled=True)  310 us
    dot_general x3, matrix products, local(): back = jnp.dot(left_scale, kernel, precision=lax.Precision.HIGH)  10.6 us
    dot_general x2, matrix products, local(): lax.dot_general(right_scale, kernel, (((1,), (1,)), ((), ())), precision=...  8.2 us

profile of v1, /device:TPU:33, one launch (start us, length us, event | category | flops | bytes accessed | tf_op | source)
XLA Modules:
  0.0 334.4 jit_solution(11567736177359802178)
XLA Ops:
  0.6 0.0 copy-start.1
  0.6 2.5 reduce_sum.126
  3.1 0.0 copy-start
  3.2 48.6 %all_to_all.80 = f32[8,4,128]{2,1,0:T(4,128)S(1)} all-to-all(f32[8,4,128]{2,1,0:T(4,128)S(1)} %broadcast_in_dim.30), channel_id=1, replica_groups=mesh['groups'=2,'far'=8,'near'=4,'col'=4,'rep'=2] {'col','rep'}, dimensions={0} | all-to-all | bytes 32768 | tf_op jit(solution)/shard_map/all_to_all | solution.py:11
  51.8 0.0 copy-done.1
  51.8 3.5 %convolution_bitcast_fusion.2 = f32[4,8,2048]{2,1,0:T(8,128)S(1)} fusion(f32[512,2048]{1,0:T(8,128)} %param.3, f32[32,512]{1,0:T(8,128)S(1)} %copy-done.1, f32[512]{0:T(512)S(1)} %bitcast.45), kind=kOutput, calls=%fused_computation.2 | convolution fusion | flops 201342976 | bytes 4524032 | tf_op jit(solution)/shard_map/dot_general | solution.py:52
  55.3 9.4 %all_to_all.81 = f32[4,8,2048]{2,1,0:T(8,128)S(1)} all-to-all(f32[4,8,2048]{2,1,0:T(8,128)S(1)} %convolution_bitcast_fusion.2), channel_id=1, replica_groups=mesh['groups'=2,'far'=8,'near'=4,'col'=4,'rep'=2] {'near'}, dimensions={0} | all-to-all | bytes 524288 | tf_op jit(solution)/shard_map/all_to_all | solution.py:11
  64.8 31.5 %all_to_all.82 = f32[8,8,256]{2,1,0:T(8,128)S(1)} all-to-all(f32[8,8,256]{2,1,0:T(8,128)S(1)} %bitcast.42), channel_id=1, replica_groups=mesh['groups'=2,'far'=8,'near'=4,'col'=4,'rep'=2] {'far'}, dimensions={0} | all-to-all | bytes 131072 | tf_op jit(solution)/shard_map/all_to_all | solution.py:11
  96.3 24.7 %all_to_all.83 = f32[8,8,256]{2,1,0:T(8,128)S(1)} all-to-all(f32[8,8,256]{2,1,0:T(8,128)S(1)} %broadcast_in_dim.31), channel_id=1, replica_groups=mesh['groups'=2,'far'=8,'near'=4,'col'=4,'rep'=2] {'far'}, dimensions={0} | all-to-all | bytes 131072 | tf_op jit(solution)/shard_map/all_to_all | solution.py:11
  121.0 8.4 %all_to_all.84 = f32[4,8,8,256]{3,2,1,0:T(8,128)S(1)} all-to-all(f32[4,8,8,256]{3,2,1,0:T(8,128)S(1)} %broadcast_in_dim.32), channel_id=1, replica_groups=mesh['groups'=2,'far'=8,'near'=4,'col'=4,'rep'=2] {'near'}, dimensions={0} | all-to-all | bytes 524288 | tf_op jit(solution)/shard_map/all_to_all | solution.py:11
  129.4 0.0 copy-done
  129.5 4.1 %fusion.3 = f32[32,512]{1,0:T(8,128)S(1)} fusion(f32[32,2048]{1,0:T(8,128)S(1)} %div.34, f32[512,2048]{1,0:T(8,128)} %param.3), kind=kOutput, calls=%fused_computation.11 | convolution fusion | flops 201326592 | bytes 4521984 | tf_op jit(solution)/shard_map/dot_general | solution.py:47
  133.6 0.1 broadcast_in_dim.33
  133.7 18.3 %all_to_all.85 = f32[8,32,512]{2,1,0:T(8,128)S(1)} all-to-all(f32[8,32,512]{2,1,0:T(8,128)S(1)} %broadcast_in_dim.33), channel_id=1, replica_groups=mesh['groups'=2,'far'=8,'near'=4,'col'=4,'rep'=2] {'col','rep'}, dimensions={0} | all-to-all | bytes 1048576 | tf_op jit(solution)/shard_map/all_to_all | solution.py:11
  152.0 3.5 %convolution_bitcast_fusion.1 = f32[4,8,2048]{2,1,0:T(8,128)S(1)} fusion(f32[512,2048]{1,0:T(8,128)} %param.3, f32[32,512]{1,0:T(8,128)S(1)} %copy-done.1, f32[32,512]{1,0:T(8,128)S(1)} %reduce_sum.130), kind=kOutput, calls=%fused_computation.1 | convolution fusion | flops 201342976 | bytes 4587520 | tf_op jit(solution)/shard_map/dot_general | solution.py:52
  155.6 8.5 %all_to_all.86 = f32[4,8,2048]{2,1,0:T(8,128)S(1)} all-to-all(f32[4,8,2048]{2,1,0:T(8,128)S(1)} %convolution_bitcast_fusion.1), channel_id=1, replica_groups=mesh['groups'=2,'far'=8,'near'=4,'col'=4,'rep'=2] {'near'}, dimensions={0} | all-to-all | bytes 524288 | tf_op jit(solution)/shard_map/all_to_all | solution.py:11
  164.1 27.1 %all_to_all.87 = f32[8,8,256]{2,1,0:T(8,128)S(1)} all-to-all(f32[8,8,256]{2,1,0:T(8,128)S(1)} %bitcast.43), channel_id=1, replica_groups=mesh['groups'=2,'far'=8,'near'=4,'col'=4,'rep'=2] {'far'}, dimensions={0} | all-to-all | bytes 131072 | tf_op jit(solution)/shard_map/all_to_all | solution.py:11
  191.2 24.2 %all_to_all.88 = f32[8,8,256]{2,1,0:T(8,128)S(1)} all-to-all(f32[8,8,256]{2,1,0:T(8,128)S(1)} %broadcast_in_dim.34), channel_id=1, replica_groups=mesh['groups'=2,'far'=8,'near'=4,'col'=4,'rep'=2] {'far'}, dimensions={0} | all-to-all | bytes 131072 | tf_op jit(solution)/shard_map/all_to_all | solution.py:11
  215.5 8.5 %all_to_all.89 = f32[4,8,8,256]{3,2,1,0:T(8,128)S(1)} all-to-all(f32[4,8,8,256]{3,2,1,0:T(8,128)S(1)} %broadcast_in_dim.35), channel_id=1, replica_groups=mesh['groups'=2,'far'=8,'near'=4,'col'=4,'rep'=2] {'near'}, dimensions={0} | all-to-all | bytes 524288 | tf_op jit(solution)/shard_map/all_to_all | solution.py:11
  224.0 4.1 %fusion.4 = f32[32,512]{1,0:T(8,128)S(1)} fusion(f32[32,2048]{1,0:T(8,128)S(1)} %div.36, f32[512,2048]{1,0:T(8,128)} %param.3), kind=kOutput, calls=%fused_computation.12 | convolution fusion | flops 201326592 | bytes 4521984 | tf_op jit(solution)/shard_map/dot_general | solution.py:47
  228.1 0.1 broadcast_in_dim.36
  228.2 18.8 %all_to_all.90 = f32[8,32,512]{2,1,0:T(8,128)S(1)} all-to-all(f32[8,32,512]{2,1,0:T(8,128)S(1)} %broadcast_in_dim.36), channel_id=1, replica_groups=mesh['groups'=2,'far'=8,'near'=4,'col'=4,'rep'=2] {'col','rep'}, dimensions={0} | all-to-all | bytes 1048576 | tf_op jit(solution)/shard_map/all_to_all | solution.py:11
  247.1 0.0 copy-start.2
  247.1 3.5 %convolution_bitcast_fusion = f32[4,8,2048]{2,1,0:T(8,128)S(1)} fusion(f32[32,512]{1,0:T(8,128)S(1)} %div.37, f32[512,2048]{1,0:T(8,128)} %param.3), kind=kOutput, calls=%fused_computation | convolution fusion | flops 201326592 | bytes 4521984 | tf_op jit(solution)/shard_map/dot_general | solution.py:52
  250.6 8.5 %all_to_all.91 = f32[4,8,2048]{2,1,0:T(8,128)S(1)} all-to-all(f32[4,8,2048]{2,1,0:T(8,128)S(1)} %convolution_bitcast_fusion), channel_id=1, replica_groups=mesh['groups'=2,'far'=8,'near'=4,'col'=4,'rep'=2] {'near'}, dimensions={0} | all-to-all | bytes 524288 | tf_op jit(solution)/shard_map/all_to_all | solution.py:11
  259.2 27.1 %all_to_all.92 = f32[8,8,256]{2,1,0:T(8,128)S(1)} all-to-all(f32[8,8,256]{2,1,0:T(8,128)S(1)} %bitcast.44), channel_id=1, replica_groups=mesh['groups'=2,'far'=8,'near'=4,'col'=4,'rep'=2] {'far'}, dimensions={0} | all-to-all | bytes 131072 | tf_op jit(solution)/shard_map/all_to_all | solution.py:11
  286.3 24.2 %all_to_all.93 = f32[8,8,256]{2,1,0:T(8,128)S(1)} all-to-all(f32[8,8,256]{2,1,0:T(8,128)S(1)} %broadcast_in_dim.37), channel_id=1, replica_groups=mesh['groups'=2,'far'=8,'near'=4,'col'=4,'rep'=2] {'far'}, dimensions={0} | all-to-all | bytes 131072 | tf_op jit(solution)/shard_map/all_to_all | solution.py:11
  310.5 8.5 %all_to_all.94 = f32[4,8,8,256]{3,2,1,0:T(8,128)S(1)} all-to-all(f32[4,8,8,256]{3,2,1,0:T(8,128)S(1)} %broadcast_in_dim.38), channel_id=1, replica_groups=mesh['groups'=2,'far'=8,'near'=4,'col'=4,'rep'=2] {'near'}, dimensions={0} | all-to-all | bytes 524288 | tf_op jit(solution)/shard_map/all_to_all | solution.py:11
  319.1 1.0 abs_reduce_fusion.2
  320.0 0.0 copy-done.2
  320.1 13.7 %all_to_all.95 = f32[8,3,32]{2,1,0:T(4,128)S(1)} all-to-all(f32[8,3,32]{2,1,0:T(4,128)S(1)} %broadcast_in_dim.39), channel_id=1, replica_groups=mesh['groups'=2,'far'=8,'near'=4,'col'=4,'rep'=2] {'col','rep'}, dimensions={0} | all-to-all | bytes 6144 | tf_op jit(solution)/shard_map/all_to_all | solution.py:11
  333.8 0.6 broadcast_multiply_fusion
  (22 shorter events, 0.4 us)
Async XLA Ops:
  0.6 51.2 %copy-start.1 = (f32[32,512]{1,0:T(8,128)S(1)}, f32[32,512]{1,0:T(8,128)}, u32[]{:S(2)}) copy-start(f32[32,512]{1,0:T(8,128)} %param.4) | copy-start | bytes 196612
  3.1 126.3 %copy-start = (f32[32,2048]{1,0:T(8,128)S(1)}, f32[32,2048]{1,0:T(8,128)}, u32[]{:S(2)}) copy-start(f32[32,2048]{1,0:T(8,128)} %param.5) | copy-start | bytes 786436
  247.1 73.0 %copy-start.2 = (f32[32,512]{1,0:T(8,128)}, f32[32,512]{1,0:T(8,128)S(1)}, u32[]{:S(2)}) copy-start(f32[32,512]{1,0:T(8,128)S(1)} %div.37) | copy-start | bytes 196612

commit v2 on v1

v2 whole, which is shorter than its diff:
```python
import jax
import jax.numpy as jnp
from jax import lax
from jax.experimental import pallas as pl
from jax.experimental.pallas import tpu as pltpu
from jax.sharding import Mesh, PartitionSpec as P

ITERS = 3
NEAR = 8
SPLIT_STEPS = 4
LANES = 128
f32 = jnp.float32
bf16 = jnp.bfloat16
WHOLE = pl.BlockSpec(memory_space=pltpu.VMEM)
PARAMS = pltpu.CompilerParams(vmem_limit_bytes=8 * 2**20)
BY_LAST = (((1,), (1,)), ((), ()))


def halves(array):
    high = array.astype(bf16)
    return high, (array - high.astype(f32)).astype(bf16)


def cost(flops, *arrays):
    moved = sum(a.size * a.dtype.itemsize for a in arrays)
    return pl.CostEstimate(flops=flops, bytes_accessed=moved, transcendentals=0)


def split_body(kernel_ref, halves_ref, sums_ref):
    kernel = kernel_ref[...]
    halves_ref[0], halves_ref[1] = halves(kernel)
    part = kernel[:, :LANES]
    for start in range(LANES, kernel.shape[1], LANES):
        part = part + kernel[:, start : start + LANES]
    sums_ref[...] = jnp.sum(part.T, axis=0, keepdims=True)


def split(kernel):
    rows, columns = kernel.shape
    tile = rows // SPLIT_STEPS
    block = pl.BlockSpec((tile, columns), lambda i: (i, 0))
    return pl.pallas_call(
        split_body,
        grid=(SPLIT_STEPS,),
        in_specs=[block],
        out_specs=[
            pl.BlockSpec((2, tile, columns), lambda i: (0, i, 0)),
            pl.BlockSpec((1, tile), lambda i: (0, i)),
        ],
        out_shape=[
            jax.ShapeDtypeStruct((2, rows, columns), bf16),
            jax.ShapeDtypeStruct((1, rows), f32),
        ],
        compiler_params=PARAMS,
        cost_estimate=cost(4 * kernel.size, kernel, kernel),
        name="split",
    )(kernel)


def back_body(value_ref, source_ref, halves_ref, left_ref, back_ref):
    value = value_ref[0]
    for i in range(1, value_ref.shape[0]):
        value = value + value_ref[i]
    left = source_ref[...] / value
    left_ref[...] = left
    high, low = halves(left)
    both = jnp.concatenate([high, low], axis=0)
    pairs = left.shape[0]
    width = back_ref.shape[2]
    for m in range(back_ref.shape[0]):
        here = slice(m * width, (m + 1) * width)
        first = jnp.dot(both, halves_ref[0, :, here], preferred_element_type=f32)
        second = jnp.dot(high, halves_ref[1, :, here], preferred_element_type=f32)
        back_ref[m] = first[:pairs] + first[pairs:] + second


def scale_left(values, source, split_kernel):
    pairs, rows = source.shape
    columns = split_kernel.shape[2]
    pieces = jax.ShapeDtypeStruct((NEAR, pairs, columns // NEAR), f32)
    return pl.pallas_call(
        back_body,
        in_specs=[WHOLE] * 3,
        out_specs=[WHOLE] * 2,
        out_shape=[jax.ShapeDtypeStruct((pairs, rows), f32), pieces],
        compiler_params=PARAMS,
        cost_estimate=cost(3 * pairs * split_kernel.size, values, source, split_kernel, pieces),
        name="back",
    )(values, source, split_kernel)


def new_right(total_ref, target_ref, old_ref, right_ref, error_ref):
    pairs = target_ref.shape[0]
    width = total_ref.shape[2]
    error = jnp.zeros((pairs, width), f32)
    for m in range(total_ref.shape[0]):
        here = slice(m * width, (m + 1) * width)
        total = total_ref[m]
        target = target_ref[:, here]
        right_ref[:, here] = target / total
        error = error + jnp.abs(old_ref[:, here] * total - target)
    error_ref[...] = jnp.sum(error, axis=1, keepdims=True)


def value_body(total_ref, target_ref, old_ref, halves_ref, right_ref, error_ref, value_ref):
    new_right(total_ref, target_ref, old_ref, right_ref, error_ref)
    pairs = target_ref.shape[0]
    high, low = halves(right_ref[...])
    both = jnp.concatenate([high, low], axis=0)
    first = lax.dot_general(both, halves_ref[0], BY_LAST, preferred_element_type=f32)
    second = lax.dot_general(high, halves_ref[1], BY_LAST, preferred_element_type=f32)
    value = first[:pairs] + first[pairs:] + second
    for i in range(value_ref.shape[0]):
        value_ref[i] = value


def scale_right(totals, target, old, split_kernel=None, copies=1):
    pairs = target.shape[0]
    out = [jax.ShapeDtypeStruct(target.shape, f32), jax.ShapeDtypeStruct((pairs, 1), f32)]
    operands = [totals, target, old]
    flops = 4 * target.size
    if split_kernel is not None:
        operands += [split_kernel]
        out += [jax.ShapeDtypeStruct((copies, pairs, split_kernel.shape[1]), f32)]
        flops += 3 * pairs * split_kernel.size
    return pl.pallas_call(
        new_right if split_kernel is None else value_body,
        in_specs=[WHOLE] * len(operands),
        out_specs=[WHOLE] * len(out),
        out_shape=out,
        compiler_params=PARAMS,
        cost_estimate=cost(flops, *operands, *out),
        name="right" if split_kernel is None else "value",
    )(*operands)


def sum_body(pieces_ref, copies_ref):
    total = pieces_ref[0]
    for i in range(1, pieces_ref.shape[0]):
        total = total + pieces_ref[i]
    for i in range(copies_ref.shape[0]):
        copies_ref[i] = total


def summed(pieces, copies):
    out = jax.ShapeDtypeStruct((copies, *pieces.shape[1:]), f32)
    return pl.pallas_call(
        sum_body,
        in_specs=[WHOLE],
        out_specs=WHOLE,
        out_shape=out,
        compiler_params=PARAMS,
        cost_estimate=cost(pieces.size, pieces, out),
        name="sum",
    )(pieces)


def exchange(pieces, axis):
    return lax.all_to_all(pieces, axis, split_axis=0, concat_axis=0, tiled=True)


def from_everyone(array, axis, size):
    return exchange(jnp.broadcast_to(array, (size, *array.shape)), axis)


def solution(mesh):
    shape = mesh.shape
    far = shape["row"] // NEAR
    split_mesh = Mesh(
        mesh.devices.reshape(shape["groups"], far, NEAR, shape["col"], shape["rep"]),
        ("groups", "far", "near", "col", "rep"),
    )
    block = ("col", "rep")
    blocks = shape["col"] * shape["rep"]

    def total_over_rows(pieces):
        pieces = exchange(summed(exchange(pieces, "near"), far), "far")
        return exchange(summed(pieces, NEAR), "near")

    def local(kernel, source, target):
        split_kernel, sums = split(kernel)
        values = from_everyone(sums, block, blocks)
        right_scale = jnp.ones(target.shape, f32)
        terms = []
        for step in range(ITERS):
            left_scale, pieces = scale_left(values, source, split_kernel)
            totals = total_over_rows(pieces)
            if step < ITERS - 1:
                right_scale, term, values = scale_right(
                    totals, target, right_scale, split_kernel, blocks
                )
                values = exchange(values, block)
            else:
                right_scale, term = scale_right(totals, target, right_scale)
            terms.append(term.reshape(-1))
        count = blocks * target.shape[1]
        errors = from_everyone(jnp.stack(terms), block, blocks).sum(axis=0) / count
        return left_scale, right_scale, errors

    return jax.shard_map(
        local,
        mesh=split_mesh,
        in_specs=(
            P(("groups", "far", "near"), block),
            P("groups", ("far", "near")),
            P("groups", block),
        ),
        out_specs=(P("groups", ("far", "near")), P("groups", block), P("groups", None)),
        check_vma=False,
    )
```

time: 335 us -> 321 us (0.958)
  blocking collectives: 310 us -> 288 us
  matrix products: 18.8 us -> 0 us
  waiting for transfers between devices: 0 us -> 11.7 us
  Pallas kernels: 0 us -> 9.51 us
  starting transfers between devices: 0 us -> 6.73 us
  other arithmetic: 4.34 us -> 0.95 us
    all_to_all x16 -> x12, blocking collectives: 310 us -> 288 us  [exchange(): return lax.all_to_all(pieces, axis, split_axis=0, concat_axis=0, tiled=True)]
    dot_general x5 -> x0, matrix products: 18.8 us -> none  [the longest x3 10.6 us: local(): back = jnp.dot(left_scale, kernel, precision=lax.Precision.HIGH)]
    all_to_all x0 -> x1, waiting for transfers between devices: none -> 11.7 us  [exchange(): return lax.all_to_all(pieces, axis, split_axis=0, concat_axis=0, tiled=True)]
    pallas_call x0 -> x13, Pallas kernels: none -> 9.51 us  [the longest x3 4 us: scale_left(): pl.pallas_call(back_body, in_specs=[WHOLE] * 3, out_specs=[WHOLE] * 2, ou...]
    all_to_all x0 -> x1, starting transfers between devices: none -> 6.73 us  [exchange(): return lax.all_to_all(pieces, axis, split_axis=0, concat_axis=0, tiled=True)]
    reduce_sum x11 -> x0, other arithmetic: 3.62 us -> none  [the longest x1 2.49 us: local(): partial_value = jnp.sum(kernel, axis=1).reshape(-1, 128)]
  transfers between devices with their start and end apart: 0 -> 1, of which waited for: 0 -> 1; matrix products, arithmetic and copies ran while one was open for 0% -> 0% of each run, Pallas kernels for 0% -> 0%
where the time goes in v2:
time: 321 us; the launch traced here: 320 us
  blocking collectives  288 us (90%)
  waiting for transfers between devices  11.7 us (4%)
  Pallas kernels  9.51 us (3%)
  starting transfers between devices  6.73 us (2%)
    all_to_all x12, blocking collectives, exchange(): return lax.all_to_all(pieces, axis, split_axis=0, concat_axis=0, tiled=True)  288 us
    all_to_all x1, waiting for transfers between devices, exchange(): return lax.all_to_all(pieces, axis, split_axis=0, concat_axis=0, tiled=True)  11.7 us
    all_to_all x1, starting transfers between devices, exchange(): return lax.all_to_all(pieces, axis, split_axis=0, concat_axis=0, tiled=True)  6.73 us
  transfers between devices with their start and end apart: 1, of which 1 were waited for; matrix products, arithmetic and copies ran while one was open for 0% of the time, Pallas kernels for 0%

profile of v2, /device:TPU:33, one launch (start us, length us, event | category | flops | bytes accessed | tf_op | source)
XLA Modules:
  0.0 319.9 jit_solution(3905411131648109384)
XLA Ops:
  0.6 0.0 copy-start
  0.6 2.2 copy-done
  2.8 0.0 copy-start.2
  2.8 1.1 split.1
  3.9 0.0 copy-start.1
  4.0 48.6 %all_to_all.65.value_ref = f32[8,1,512]{2,1,0:T(1,128)S(1)} all-to-all(f32[8,1,512]{2,1,0:T(1,128)S(1)} %broadcast_in_dim.9), channel_id=1, replica_groups=mesh['groups'=2,'far'=4,'near'=8,'col'=4,'rep'=2] {'col','rep'}, dimensions={0} | all-to-all | bytes 32768 | tf_op jit(solution)/shard_map/all_to_all | solution.py:159
  52.6 0.0 copy-done.2
  52.6 1.3 back.3
  53.9 16.7 %all_to_all.66.pieces_ref = f32[8,32,256]{2,1,0:T(8,128)S(1)} all-to-all(f32[8,32,256]{2,1,0:T(8,128)S(1)} %get-tuple-element.19), channel_id=1, replica_groups=mesh['groups'=2,'far'=4,'near'=8,'col'=4,'rep'=2] {'near'}, dimensions={0} | all-to-all | bytes 524288 | tf_op jit(solution)/shard_map/all_to_all | solution.py:159
  70.6 37.3 %all_to_all.67.pieces_ref = f32[4,32,256]{2,1,0:T(8,128)S(1)} all-to-all(f32[4,32,256]{2,1,0:T(8,128)S(1)} %sum.6), channel_id=1, replica_groups=mesh['groups'=2,'far'=4,'near'=8,'col'=4,'rep'=2] {'far'}, dimensions={0} | all-to-all | bytes 262144 | tf_op jit(solution)/shard_map/all_to_all | solution.py:159
  107.9 18.4 %all_to_all.68.total_ref = f32[8,32,256]{2,1,0:T(8,128)S(1)} all-to-all(f32[8,32,256]{2,1,0:T(8,128)S(1)} %sum.7), channel_id=1, replica_groups=mesh['groups'=2,'far'=4,'near'=8,'col'=4,'rep'=2] {'near'}, dimensions={0} | all-to-all | bytes 524288 | tf_op jit(solution)/shard_map/all_to_all | solution.py:159
  126.3 0.0 copy-done.1
  126.3 1.4 value.2
  127.7 18.8 %all_to_all.69.value_ref = f32[8,32,512]{2,1,0:T(8,128)S(1)} all-to-all(f32[8,32,512]{2,1,0:T(8,128)S(1)} %get-tuple-element.20), channel_id=1, replica_groups=mesh['groups'=2,'far'=4,'near'=8,'col'=4,'rep'=2] {'col','rep'}, dimensions={0} | all-to-all | bytes 1048576 | tf_op jit(solution)/shard_map/all_to_all | solution.py:159
  146.5 1.3 back.4
  147.8 15.8 %all_to_all.70.pieces_ref = f32[8,32,256]{2,1,0:T(8,128)S(1)} all-to-all(f32[8,32,256]{2,1,0:T(8,128)S(1)} %get-tuple-element.21), channel_id=1, replica_groups=mesh['groups'=2,'far'=4,'near'=8,'col'=4,'rep'=2] {'near'}, dimensions={0} | all-to-all | bytes 524288 | tf_op jit(solution)/shard_map/all_to_all | solution.py:159
  163.7 33.2 %all_to_all.71.pieces_ref = f32[4,32,256]{2,1,0:T(8,128)S(1)} all-to-all(f32[4,32,256]{2,1,0:T(8,128)S(1)} %sum.8), channel_id=1, replica_groups=mesh['groups'=2,'far'=4,'near'=8,'col'=4,'rep'=2] {'far'}, dimensions={0} | all-to-all | bytes 262144 | tf_op jit(solution)/shard_map/all_to_all | solution.py:159
  196.9 18.4 %all_to_all.72.total_ref = f32[8,32,256]{2,1,0:T(8,128)S(1)} all-to-all(f32[8,32,256]{2,1,0:T(8,128)S(1)} %sum.9), channel_id=1, replica_groups=mesh['groups'=2,'far'=4,'near'=8,'col'=4,'rep'=2] {'near'}, dimensions={0} | all-to-all | bytes 524288 | tf_op jit(solution)/shard_map/all_to_all | solution.py:159
  215.4 1.4 value.3
  216.8 17.7 %all_to_all.73.value_ref = f32[8,32,512]{2,1,0:T(8,128)S(1)} all-to-all(f32[8,32,512]{2,1,0:T(8,128)S(1)} %get-tuple-element.23), channel_id=1, replica_groups=mesh['groups'=2,'far'=4,'near'=8,'col'=4,'rep'=2] {'col','rep'}, dimensions={0} | all-to-all | bytes 1048576 | tf_op jit(solution)/shard_map/all_to_all | solution.py:159
  234.4 1.3 back.5
  235.8 16.4 %all_to_all.74.pieces_ref = f32[8,32,256]{2,1,0:T(8,128)S(1)} all-to-all(f32[8,32,256]{2,1,0:T(8,128)S(1)} %get-tuple-element.25), channel_id=1, replica_groups=mesh['groups'=2,'far'=4,'near'=8,'col'=4,'rep'=2] {'near'}, dimensions={0} | all-to-all | bytes 524288 | tf_op jit(solution)/shard_map/all_to_all | solution.py:159
  252.1 33.9 %all_to_all.75.pieces_ref = f32[4,32,256]{2,1,0:T(8,128)S(1)} all-to-all(f32[4,32,256]{2,1,0:T(8,128)S(1)} %sum.10), channel_id=1, replica_groups=mesh['groups'=2,'far'=4,'near'=8,'col'=4,'rep'=2] {'far'}, dimensions={0} | all-to-all | bytes 262144 | tf_op jit(solution)/shard_map/all_to_all | solution.py:159
  286.0 0.7 sum.11
  286.8 6.7 %all-to-all-start.11 = ((f32[8,32,256]{2,1,0:T(8,128)}), f32[8,32,256]{2,1,0:T(8,128)S(1)}, u32[]{:S(2)}, u32[]{:S(2)}) async-start(f32[8,32,256]{2,1,0:T(8,128)} %sum.11), calls=%async_computation.11 | async-start | bytes 524288 | tf_op jit(solution)/shard_map/all_to_all | solution.py:159
  293.5 0.1 reduce
  293.6 0.1 reduce.1
  293.7 11.7 %all-to-all-done.11.total_ref = f32[8,32,256]{2,1,0:T(8,128)S(1)} async-done(((f32[8,32,256]{2,1,0:T(8,128)}), f32[8,32,256]{2,1,0:T(8,128)S(1)}, u32[]{:S(2)}, u32[]{:S(2)}) %all-to-all-start.11) | async-done | bytes 262176 | tf_op jit(solution)/shard_map/all_to_all | solution.py:159
  305.4 0.8 right.1
  306.2 0.1 reduce.2
  306.3 13.0 %all_to_all.76 = f32[8,3,32]{2,1,0:T(4,128)S(1)} all-to-all(f32[8,3,32]{2,1,0:T(4,128)S(1)} %broadcast_in_dim.11), channel_id=1, replica_groups=mesh['groups'=2,'far'=4,'near'=8,'col'=4,'rep'=2] {'col','rep'}, dimensions={0} | all-to-all | bytes 6144 | tf_op jit(solution)/shard_map/all_to_all | solution.py:159
  319.3 0.6 broadcast_multiply_fusion
  (10 shorter events, 0.2 us)
Async XLA Ops:
  0.6 2.2 copy-start
  2.8 49.8 %copy-start.2 = (f32[32,512]{1,0:T(8,128)S(1)}, f32[32,512]{1,0:T(8,128)}, u32[]{:S(2)}) copy-start(f32[32,512]{1,0:T(8,128)} %source_ref.5) | copy-start | bytes 196612
  3.9 122.4 %copy-start.1 = (f32[32,2048]{1,0:T(8,128)S(1)}, f32[32,2048]{1,0:T(8,128)}, u32[]{:S(2)}) copy-start(f32[32,2048]{1,0:T(8,128)} %target_ref.5) | copy-start | bytes 786436
  286.8 18.7 %all-to-all-start.11 = ((f32[8,32,256]{2,1,0:T(8,128)}), f32[8,32,256]{2,1,0:T(8,128)S(1)}, u32[]{:S(2)}, u32[]{:S(2)}) async-start(f32[8,32,256]{2,1,0:T(8,128)} %sum.11), calls=%async_computation.11 | async-start | bytes 524288 | tf_op jit(solution)/shard_map/all_to_all | solution.py:159

commit v3 on v2

--- a/solution.py
+++ b/solution.py
@@ -3,7 +3,7 @@
 from jax import lax
 from jax.experimental import pallas as pl
 from jax.experimental.pallas import tpu as pltpu
-from jax.sharding import Mesh, PartitionSpec as P
+from jax.sharding import PartitionSpec as P
 
 ITERS = 3
 NEAR = 8
@@ -155,8 +155,10 @@
     )(pieces)
 
 
-def exchange(pieces, axis):
-    return lax.all_to_all(pieces, axis, split_axis=0, concat_axis=0, tiled=True)
+def exchange(pieces, axis, groups=None):
+    return lax.all_to_all(
+        pieces, axis, split_axis=0, concat_axis=0, tiled=True, axis_index_groups=groups
+    )
 
 
 def from_everyone(array, axis, size):
@@ -164,18 +166,30 @@
 
 
 def solution(mesh):
-    shape = mesh.shape
-    far = shape["row"] // NEAR
-    split_mesh = Mesh(
-        mesh.devices.reshape(shape["groups"], far, NEAR, shape["col"], shape["rep"]),
-        ("groups", "far", "near", "col", "rep"),
-    )
+    rows, cores = mesh.shape["row"], mesh.shape["rep"]
+    far = rows // NEAR
     block = ("col", "rep")
-    blocks = shape["col"] * shape["rep"]
+    blocks = mesh.shape["col"] * cores
+    lines = ("row", "rep")
+
+    def device(row, core):
+        return (row + core * NEAR // cores) % rows * cores + core
+
+    near_groups = [
+        [device(start + i, core) for i in range(NEAR)]
+        for core in range(cores)
+        for start in range(0, rows, NEAR)
+    ]
+    far_groups = [
+        [device(start + i, core) for start in range(0, rows, NEAR)]
+        for core in range(cores)
+        for i in range(NEAR)
+    ]
 
     def total_over_rows(pieces):
-        pieces = exchange(summed(exchange(pieces, "near"), far), "far")
-        return exchange(summed(pieces, NEAR), "near")
+        pieces = summed(exchange(pieces, lines, near_groups), far)
+        pieces = summed(exchange(pieces, lines, far_groups), NEAR)
+        return exchange(pieces, lines, near_groups)
 
     def local(kernel, source, target):
         split_kernel, sums = split(kernel)
@@ -199,12 +213,8 @@
 
     return jax.shard_map(
         local,
-        mesh=split_mesh,
-        in_specs=(
-            P(("groups", "far", "near"), block),
-            P("groups", ("far", "near")),
-            P("groups", block),
-        ),
-        out_specs=(P("groups", ("far", "near")), P("groups", block), P("groups", None)),
+        mesh=mesh,
+        in_specs=(P(("groups", "row"), block), P("groups", "row"), P("groups", block)),
+        out_specs=(P("groups", "row"), P("groups", block), P("groups", None)),
         check_vma=False,
     )

time: 321 us -> 314 us (0.978)
  blocking collectives: 288 us -> 281 us
  starting transfers between devices: 6.73 us -> 12.9 us
  waiting for transfers between devices: 11.7 us -> 5.85 us
    all_to_all x12, blocking collectives: 288 us -> 281 us  [exchange(): lax.all_to_all(pieces, axis, split_axis=0, concat_axis=0, tiled=True, axi...]
    all_to_all x1, starting transfers between devices: 6.73 us -> 12.9 us  [exchange(): lax.all_to_all(pieces, axis, split_axis=0, concat_axis=0, tiled=True, axi...]
    all_to_all x1, waiting for transfers between devices: 11.7 us -> 5.85 us  [exchange(): lax.all_to_all(pieces, axis, split_axis=0, concat_axis=0, tiled=True, axi...]
where the time goes in v3:
time: 314 us; the launch traced here: 313 us
  blocking collectives  281 us (89%)
  starting transfers between devices  12.9 us (4%)
  Pallas kernels  9.51 us (3%)
  waiting for transfers between devices  5.85 us (2%)
    all_to_all x12, blocking collectives, exchange(): lax.all_to_all(pieces, axis, split_axis=0, concat_axis=0, tiled=True, axi...  281 us
    all_to_all x1, starting transfers between devices, exchange(): lax.all_to_all(pieces, axis, split_axis=0, concat_axis=0, tiled=True, axi...  12.9 us
  transfers between devices with their start and end apart: 1, of which 1 were waited for; matrix products, arithmetic and copies ran while one was open for 0% of the time, Pallas kernels for 0%

profile of v3, /device:TPU:33, one launch (start us, length us, event | category | flops | bytes accessed | tf_op | source)
XLA Modules:
  0.0 313.3 jit_solution(15070242204034732981)
XLA Ops:
  0.6 0.0 copy-start
  0.6 2.2 copy-done
  2.8 0.0 copy-start.2
  2.8 1.1 split.1
  3.9 0.0 copy-start.1
  4.0 48.6 %all_to_all.65.value_ref = f32[8,1,512]{2,1,0:T(1,128)S(1)} all-to-all(f32[8,1,512]{2,1,0:T(1,128)S(1)} %broadcast_in_dim.9), channel_id=1, replica_groups=mesh['groups'=2,'row'=32,'col'=4,'rep'=2] {'col','rep'}, dimensions={0} | all-to-all | bytes 32768 | tf_op jit(solution)/shard_map/all_to_all | solution.py:159
  52.6 0.0 copy-done.2
  52.6 1.3 back.3
  53.9 17.1 %all_to_all.66.pieces_ref = f32[8,32,256]{2,1,0:T(8,128)S(1)} all-to-all(f32[8,32,256]{2,1,0:T(8,128)S(1)} %get-tuple-element.19), channel_id=1, replica_groups={{0,8,16,24,32,40,48,56},{64,72,80,88,96,104,112,120},{128,136,144,152,1..., dimensions={0} | all-to-all | bytes 524288 | tf_op jit(solution)/shard_map/all_to_all | solution.py:159
  71.0 35.1 %all_to_all.67.pieces_ref = f32[4,32,256]{2,1,0:T(8,128)S(1)} all-to-all(f32[4,32,256]{2,1,0:T(8,128)S(1)} %sum.6), channel_id=1, replica_groups={{0,64,128,192},{8,72,136,200},{16,80,144,208},{24,88,152,216},{32,96,16..., dimensions={0} | all-to-all | bytes 262144 | tf_op jit(solution)/shard_map/all_to_all | solution.py:159
  106.2 15.3 %all_to_all.68.total_ref = f32[8,32,256]{2,1,0:T(8,128)S(1)} all-to-all(f32[8,32,256]{2,1,0:T(8,128)S(1)} %sum.7), channel_id=1, replica_groups={{0,8,16,24,32,40,48,56},{64,72,80,88,96,104,112,120},{128,136,144,152,1..., dimensions={0} | all-to-all | bytes 524288 | tf_op jit(solution)/shard_map/all_to_all | solution.py:159
  121.5 0.0 copy-done.1
  121.5 1.4 value.2
  122.9 21.6 %all_to_all.69.value_ref = f32[8,32,512]{2,1,0:T(8,128)S(1)} all-to-all(f32[8,32,512]{2,1,0:T(8,128)S(1)} %get-tuple-element.20), channel_id=1, replica_groups=mesh['groups'=2,'row'=32,'col'=4,'rep'=2] {'col','rep'}, dimensions={0} | all-to-all | bytes 1048576 | tf_op jit(solution)/shard_map/all_to_all | solution.py:159
  144.5 1.3 back.4
  145.9 17.3 %all_to_all.70.pieces_ref = f32[8,32,256]{2,1,0:T(8,128)S(1)} all-to-all(f32[8,32,256]{2,1,0:T(8,128)S(1)} %get-tuple-element.21), channel_id=1, replica_groups={{0,8,16,24,32,40,48,56},{64,72,80,88,96,104,112,120},{128,136,144,152,1..., dimensions={0} | all-to-all | bytes 524288 | tf_op jit(solution)/shard_map/all_to_all | solution.py:159
  163.2 28.6 %all_to_all.71.pieces_ref = f32[4,32,256]{2,1,0:T(8,128)S(1)} all-to-all(f32[4,32,256]{2,1,0:T(8,128)S(1)} %sum.8), channel_id=1, replica_groups={{0,64,128,192},{8,72,136,200},{16,80,144,208},{24,88,152,216},{32,96,16..., dimensions={0} | all-to-all | bytes 262144 | tf_op jit(solution)/shard_map/all_to_all | solution.py:159
  191.9 19.6 %all_to_all.72.total_ref = f32[8,32,256]{2,1,0:T(8,128)S(1)} all-to-all(f32[8,32,256]{2,1,0:T(8,128)S(1)} %sum.9), channel_id=1, replica_groups={{0,8,16,24,32,40,48,56},{64,72,80,88,96,104,112,120},{128,136,144,152,1..., dimensions={0} | all-to-all | bytes 524288 | tf_op jit(solution)/shard_map/all_to_all | solution.py:159
  211.5 1.4 value.3
  212.9 16.9 %all_to_all.73.value_ref = f32[8,32,512]{2,1,0:T(8,128)S(1)} all-to-all(f32[8,32,512]{2,1,0:T(8,128)S(1)} %get-tuple-element.23), channel_id=1, replica_groups=mesh['groups'=2,'row'=32,'col'=4,'rep'=2] {'col','rep'}, dimensions={0} | all-to-all | bytes 1048576 | tf_op jit(solution)/shard_map/all_to_all | solution.py:159
  229.8 1.3 back.5
  231.1 15.1 %all_to_all.74.pieces_ref = f32[8,32,256]{2,1,0:T(8,128)S(1)} all-to-all(f32[8,32,256]{2,1,0:T(8,128)S(1)} %get-tuple-element.25), channel_id=1, replica_groups={{0,8,16,24,32,40,48,56},{64,72,80,88,96,104,112,120},{128,136,144,152,1..., dimensions={0} | all-to-all | bytes 524288 | tf_op jit(solution)/shard_map/all_to_all | solution.py:159
  246.2 25.2 %all_to_all.75.pieces_ref = f32[4,32,256]{2,1,0:T(8,128)S(1)} all-to-all(f32[4,32,256]{2,1,0:T(8,128)S(1)} %sum.10), channel_id=1, replica_groups={{0,64,128,192},{8,72,136,200},{16,80,144,208},{24,88,152,216},{32,96,16..., dimensions={0} | all-to-all | bytes 262144 | tf_op jit(solution)/shard_map/all_to_all | solution.py:159
  271.5 0.7 sum.11
  272.2 12.9 %all-to-all-start.11 = ((f32[8,32,256]{2,1,0:T(8,128)}), f32[8,32,256]{2,1,0:T(8,128)S(1)}, u32[]{:S(2)}, u32[]{:S(2)}) async-start(f32[8,32,256]{2,1,0:T(8,128)} %sum.11), calls=%async_computation.11 | async-start | bytes 524288 | tf_op jit(solution)/shard_map/all_to_all | solution.py:159
  285.1 0.1 reduce
  285.2 0.1 reduce.1
  285.3 5.9 %all-to-all-done.11.total_ref = f32[8,32,256]{2,1,0:T(8,128)S(1)} async-done(((f32[8,32,256]{2,1,0:T(8,128)}), f32[8,32,256]{2,1,0:T(8,128)S(1)}, u32[]{:S(2)}, u32[]{:S(2)}) %all-to-all-start.11) | async-done | bytes 262176 | tf_op jit(solution)/shard_map/all_to_all | solution.py:159
  291.1 0.8 right.1
  291.9 0.1 reduce.2
  292.1 20.6 %all_to_all.76 = f32[8,3,32]{2,1,0:T(4,128)S(1)} all-to-all(f32[8,3,32]{2,1,0:T(4,128)S(1)} %broadcast_in_dim.11), channel_id=1, replica_groups=mesh['groups'=2,'row'=32,'col'=4,'rep'=2] {'col','rep'}, dimensions={0} | all-to-all | bytes 6144 | tf_op jit(solution)/shard_map/all_to_all | solution.py:159
  312.7 0.6 broadcast_multiply_fusion
  (10 shorter events, 0.2 us)
Async XLA Ops:
  0.6 2.2 copy-start
  2.8 49.8 %copy-start.2 = (f32[32,512]{1,0:T(8,128)S(1)}, f32[32,512]{1,0:T(8,128)}, u32[]{:S(2)}) copy-start(f32[32,512]{1,0:T(8,128)} %source_ref.5) | copy-start | bytes 196612
  3.9 117.6 %copy-start.1 = (f32[32,2048]{1,0:T(8,128)S(1)}, f32[32,2048]{1,0:T(8,128)}, u32[]{:S(2)}) copy-start(f32[32,2048]{1,0:T(8,128)} %target_ref.5) | copy-start | bytes 786436
  272.2 18.9 %all-to-all-start.11 = ((f32[8,32,256]{2,1,0:T(8,128)}), f32[8,32,256]{2,1,0:T(8,128)S(1)}, u32[]{:S(2)}, u32[]{:S(2)}) async-start(f32[8,32,256]{2,1,0:T(8,128)} %sum.11), calls=%async_computation.11 | async-start | bytes 524288 | tf_op jit(solution)/shard_map/all_to_all | solution.py:159

commit v4 on v3

--- a/solution.py
+++ b/solution.py
@@ -1,3 +1,5 @@
+import functools
+
 import jax
 import jax.numpy as jnp
 from jax import lax
@@ -9,6 +11,7 @@
 NEAR = 8
 SPLIT_STEPS = 4
 LANES = 128
+SUBLANES = 8
 f32 = jnp.float32
 bf16 = jnp.bfloat16
 WHOLE = pl.BlockSpec(memory_space=pltpu.VMEM)
@@ -32,27 +35,29 @@
     part = kernel[:, :LANES]
     for start in range(LANES, kernel.shape[1], LANES):
         part = part + kernel[:, start : start + LANES]
-    sums_ref[...] = jnp.sum(part.T, axis=0, keepdims=True)
-
-
-def split(kernel):
+    sums = jnp.sum(part.T, axis=0, keepdims=True)
+    for i in range(sums_ref.shape[0]):
+        sums_ref[i] = sums
+
+
+def split(kernel, copies):
     rows, columns = kernel.shape
     tile = rows // SPLIT_STEPS
-    block = pl.BlockSpec((tile, columns), lambda i: (i, 0))
+    out = [
+        jax.ShapeDtypeStruct((2, rows, columns), bf16),
+        jax.ShapeDtypeStruct((copies, 1, rows), f32),
+    ]
     return pl.pallas_call(
         split_body,
         grid=(SPLIT_STEPS,),
-        in_specs=[block],
+        in_specs=[pl.BlockSpec((tile, columns), lambda i: (i, 0))],
         out_specs=[
             pl.BlockSpec((2, tile, columns), lambda i: (0, i, 0)),
-            pl.BlockSpec((1, tile), lambda i: (0, i)),
+            pl.BlockSpec((copies, 1, tile), lambda i: (0, 0, i)),
         ],
-        out_shape=[
-            jax.ShapeDtypeStruct((2, rows, columns), bf16),
-            jax.ShapeDtypeStruct((1, rows), f32),
-        ],
-        compiler_params=PARAMS,
-        cost_estimate=cost(4 * kernel.size, kernel, kernel),
+        out_shape=out,
+        compiler_params=PARAMS,
+        cost_estimate=cost(4 * kernel.size, kernel, *out),
         name="split",
     )(kernel)
 
@@ -89,7 +94,7 @@
     )(values, source, split_kernel)
 
 
-def new_right(total_ref, target_ref, old_ref, right_ref, error_ref):
+def new_right(total_ref, target_ref, old_ref, right_ref):
     pairs = target_ref.shape[0]
     width = total_ref.shape[2]
     error = jnp.zeros((pairs, width), f32)
@@ -99,11 +104,11 @@
         target = target_ref[:, here]
         right_ref[:, here] = target / total
         error = error + jnp.abs(old_ref[:, here] * total - target)
-    error_ref[...] = jnp.sum(error, axis=1, keepdims=True)
+    return jnp.sum(error, axis=1, keepdims=True)
 
 
 def value_body(total_ref, target_ref, old_ref, halves_ref, right_ref, error_ref, value_ref):
-    new_right(total_ref, target_ref, old_ref, right_ref, error_ref)
+    error_ref[...] = new_right(total_ref, target_ref, old_ref, right_ref)
     pairs = target_ref.shape[0]
     high, low = halves(right_ref[...])
     both = jnp.concatenate([high, low], axis=0)
@@ -114,23 +119,22 @@
         value_ref[i] = value
 
 
-def scale_right(totals, target, old, split_kernel=None, copies=1):
+def scale_right(totals, target, old, split_kernel, copies):
     pairs = target.shape[0]
-    out = [jax.ShapeDtypeStruct(target.shape, f32), jax.ShapeDtypeStruct((pairs, 1), f32)]
-    operands = [totals, target, old]
-    flops = 4 * target.size
-    if split_kernel is not None:
-        operands += [split_kernel]
-        out += [jax.ShapeDtypeStruct((copies, pairs, split_kernel.shape[1]), f32)]
-        flops += 3 * pairs * split_kernel.size
-    return pl.pallas_call(
-        new_right if split_kernel is None else value_body,
-        in_specs=[WHOLE] * len(operands),
-        out_specs=[WHOLE] * len(out),
-        out_shape=out,
-        compiler_params=PARAMS,
-        cost_estimate=cost(flops, *operands, *out),
-        name="right" if split_kernel is None else "value",
+    out = [
+        jax.ShapeDtypeStruct(target.shape, f32),
+        jax.ShapeDtypeStruct((pairs, 1), f32),
+        jax.ShapeDtypeStruct((copies, pairs, split_kernel.shape[1]), f32),
+    ]
+    operands = [totals, target, old, split_kernel]
+    return pl.pallas_call(
+        value_body,
+        in_specs=[WHOLE] * 4,
+        out_specs=[WHOLE] * 3,
+        out_shape=out,
+        compiler_params=PARAMS,
+        cost_estimate=cost(3 * pairs * split_kernel.size, *operands, *out),
+        name="value",
     )(*operands)
 
 
@@ -155,14 +159,61 @@
     )(pieces)
 
 
+def last_body(total_ref, target_ref, old_ref, *refs):
+    *terms, right_ref, errors_ref = refs
+    error = new_right(total_ref, target_ref, old_ref, right_ref)
+    lane = lax.broadcasted_iota(jnp.int32, (error.shape[0], LANES), 1)
+    table = jnp.zeros((error.shape[0], LANES), f32)
+    for i, term in enumerate([*(t[...] for t in terms), error]):
+        table = jnp.where(lane == i, term, table)
+    rest = jnp.zeros((LANES - table.shape[0], LANES), f32)
+    table = jnp.concatenate([table, rest], axis=0).T[: errors_ref.shape[1]]
+    for i in range(errors_ref.shape[0]):
+        errors_ref[i] = table
+
+
+def last_right(totals, target, old, terms, copies):
+    pairs = target.shape[0]
+    out = [
+        jax.ShapeDtypeStruct(target.shape, f32),
+        jax.ShapeDtypeStruct((copies, SUBLANES, LANES), f32),
+    ]
+    operands = [totals, target, old, *terms]
+    return pl.pallas_call(
+        last_body,
+        in_specs=[WHOLE] * len(operands),
+        out_specs=[WHOLE] * 2,
+        out_shape=out,
+        compiler_params=PARAMS,
+        cost_estimate=cost(4 * target.size, *operands, *out),
+        name="last",
+    )(*operands)
+
+
+def errors_body(count, tables_ref, errors_ref):
+    table = tables_ref[0]
+    for i in range(1, tables_ref.shape[0]):
+        table = table + tables_ref[i]
+    errors_ref[...] = table[: errors_ref.shape[0], : errors_ref.shape[1]] / count
+
+
+def mean_errors(tables, pairs, count):
+    out = jax.ShapeDtypeStruct((ITERS, pairs), f32)
+    return pl.pallas_call(
+        functools.partial(errors_body, count),
+        in_specs=[WHOLE],
+        out_specs=WHOLE,
+        out_shape=out,
+        compiler_params=PARAMS,
+        cost_estimate=cost(tables.size, tables, out),
+        name="errors",
+    )(tables)
+
+
 def exchange(pieces, axis, groups=None):
     return lax.all_to_all(
         pieces, axis, split_axis=0, concat_axis=0, tiled=True, axis_index_groups=groups
     )
-
-
-def from_everyone(array, axis, size):
-    return exchange(jnp.broadcast_to(array, (size, *array.shape)), axis)
 
 
 def solution(mesh):
@@ -175,25 +226,25 @@
     def device(row, core):
         return (row + core * NEAR // cores) % rows * cores + core
 
-    near_groups = [
-        [device(start + i, core) for i in range(NEAR)]
-        for core in range(cores)
-        for start in range(0, rows, NEAR)
-    ]
-    far_groups = [
-        [device(start + i, core) for start in range(0, rows, NEAR)]
-        for core in range(cores)
-        for i in range(NEAR)
-    ]
+    def groups_of(members):
+        return [[device(row, core) for row in rows_of] for core in range(cores) for rows_of in members]
+
+    half = NEAR // 2
+    starts = range(0, rows, NEAR)
+    sum_groups = groups_of([[start + i for i in range(NEAR)] for start in starts])
+    far_groups = groups_of([[start + i for start in starts] for i in range(NEAR)])
+    gather_groups = groups_of(
+        [[start + i + (NEAR if i < half else 0) for i in range(NEAR)] for start in starts]
+    )
 
     def total_over_rows(pieces):
-        pieces = summed(exchange(pieces, lines, near_groups), far)
+        pieces = summed(exchange(pieces, lines, sum_groups), far)
         pieces = summed(exchange(pieces, lines, far_groups), NEAR)
-        return exchange(pieces, lines, near_groups)
+        return exchange(pieces, lines, gather_groups)
 
     def local(kernel, source, target):
-        split_kernel, sums = split(kernel)
-        values = from_everyone(sums, block, blocks)
+        split_kernel, sums = split(kernel, blocks)
+        values = exchange(sums, block)
         right_scale = jnp.ones(target.shape, f32)
         terms = []
         for step in range(ITERS):
@@ -204,11 +255,10 @@
                     totals, target, right_scale, split_kernel, blocks
                 )
                 values = exchange(values, block)
-            else:
-                right_scale, term = scale_right(totals, target, right_scale)
-            terms.append(term.reshape(-1))
-        count = blocks * target.shape[1]
-        errors = from_everyone(jnp.stack(terms), block, blocks).sum(axis=0) / count
+                terms.append(term)
+        right_scale, tables = last_right(totals, target, right_scale, terms, blocks)
+        count = float(blocks * target.shape[1])
+        errors = mean_errors(exchange(tables, block), target.shape[0], count)
         return left_scale, right_scale, errors
 
     return jax.shard_map(

time: 314 us -> 302 us (0.962)
  starting transfers between devices: 12.9 us -> 0 us
  blocking collectives: 281 us -> 289 us
  waiting for transfers between devices: 5.85 us -> 0 us
    all_to_all x1 -> x0, starting transfers between devices: 12.9 us -> none  [exchange(): lax.all_to_all(pieces, axis, split_axis=0, concat_axis=0, tiled=True, axi...]
    all_to_all x12 -> x13, blocking collectives: 281 us -> 289 us  [exchange(): lax.all_to_all(pieces, axis, split_axis=0, concat_axis=0, tiled=True, axi...]
    all_to_all x1 -> x0, waiting for transfers between devices: 5.85 us -> none  [exchange(): lax.all_to_all(pieces, axis, split_axis=0, concat_axis=0, tiled=True, axi...]
  transfers between devices with their start and end apart: 1 -> 0, of which waited for: 1 -> 0; matrix products, arithmetic and copies ran while one was open for 0% -> 0% of each run, Pallas kernels for 0% -> 0%
where the time goes in v4:
time: 302 us; the launch traced here: 301 us
  blocking collectives  289 us (96%)
  Pallas kernels  9.38 us (3%)
    all_to_all x13, blocking collectives, exchange(): lax.all_to_all(pieces, axis, split_axis=0, concat_axis=0, tiled=True, axi...  289 us

profile of v4, /device:TPU:33, one launch (start us, length us, event | category | flops | bytes accessed | tf_op | source)
XLA Modules:
  0.0 301.1 jit_solution(7044824329819306896)
XLA Ops:
  0.6 0.0 copy-start
  0.6 2.2 copy-done
  2.8 0.0 copy-start.2
  2.8 1.1 split.1
  4.0 0.0 copy-start.1
  4.0 48.6 %all_to_all.65.value_ref = f32[8,1,512]{2,1,0:T(1,128)S(1)} all-to-all(f32[8,1,512]{2,1,0:T(1,128)S(1)} %get-tuple-element.17), channel_id=1, replica_groups=mesh['groups'=2,'row'=32,'col'=4,'rep'=2] {'col','rep'}, dimensions={0} | all-to-all | bytes 32768 | tf_op jit(solution)/shard_map/all_to_all | solution.py:214
  52.6 0.0 copy-done.2
  52.6 1.3 back.3
  53.9 17.1 %all_to_all.66.pieces_ref = f32[8,32,256]{2,1,0:T(8,128)S(1)} all-to-all(f32[8,32,256]{2,1,0:T(8,128)S(1)} %get-tuple-element.19), channel_id=1, replica_groups={{0,8,16,24,32,40,48,56},{64,72,80,88,96,104,112,120},{128,136,144,152,1..., dimensions={0} | all-to-all | bytes 524288 | tf_op jit(solution)/shard_map/all_to_all | solution.py:214
  71.0 35.1 %all_to_all.67.pieces_ref = f32[4,32,256]{2,1,0:T(8,128)S(1)} all-to-all(f32[4,32,256]{2,1,0:T(8,128)S(1)} %sum.6), channel_id=1, replica_groups={{0,64,128,192},{8,72,136,200},{16,80,144,208},{24,88,152,216},{32,96,16..., dimensions={0} | all-to-all | bytes 262144 | tf_op jit(solution)/shard_map/all_to_all | solution.py:214
  106.2 20.9 %all_to_all.68.total_ref = f32[8,32,256]{2,1,0:T(8,128)S(1)} all-to-all(f32[8,32,256]{2,1,0:T(8,128)S(1)} %sum.7), channel_id=1, replica_groups={{64,72,80,88,32,40,48,56},{128,136,144,152,96,104,112,120},{192,200,208..., dimensions={0} | all-to-all | bytes 524288 | tf_op jit(solution)/shard_map/all_to_all | solution.py:214
  127.1 0.0 copy-done.1
  127.1 1.4 value.2
  128.5 12.1 %all_to_all.69.value_ref = f32[8,32,512]{2,1,0:T(8,128)S(1)} all-to-all(f32[8,32,512]{2,1,0:T(8,128)S(1)} %get-tuple-element.20), channel_id=1, replica_groups=mesh['groups'=2,'row'=32,'col'=4,'rep'=2] {'col','rep'}, dimensions={0} | all-to-all | bytes 1048576 | tf_op jit(solution)/shard_map/all_to_all | solution.py:214
  140.6 1.3 back.4
  141.9 15.4 %all_to_all.70.pieces_ref = f32[8,32,256]{2,1,0:T(8,128)S(1)} all-to-all(f32[8,32,256]{2,1,0:T(8,128)S(1)} %get-tuple-element.21), channel_id=1, replica_groups={{0,8,16,24,32,40,48,56},{64,72,80,88,96,104,112,120},{128,136,144,152,1..., dimensions={0} | all-to-all | bytes 524288 | tf_op jit(solution)/shard_map/all_to_all | solution.py:214
  157.3 24.4 %all_to_all.71.pieces_ref = f32[4,32,256]{2,1,0:T(8,128)S(1)} all-to-all(f32[4,32,256]{2,1,0:T(8,128)S(1)} %sum.8), channel_id=1, replica_groups={{0,64,128,192},{8,72,136,200},{16,80,144,208},{24,88,152,216},{32,96,16..., dimensions={0} | all-to-all | bytes 262144 | tf_op jit(solution)/shard_map/all_to_all | solution.py:214
  181.7 21.5 %all_to_all.72.total_ref = f32[8,32,256]{2,1,0:T(8,128)S(1)} all-to-all(f32[8,32,256]{2,1,0:T(8,128)S(1)} %sum.9), channel_id=1, replica_groups={{64,72,80,88,32,40,48,56},{128,136,144,152,96,104,112,120},{192,200,208..., dimensions={0} | all-to-all | bytes 524288 | tf_op jit(solution)/shard_map/all_to_all | solution.py:214
  203.2 1.4 value.3
  204.6 18.0 %all_to_all.73.value_ref = f32[8,32,512]{2,1,0:T(8,128)S(1)} all-to-all(f32[8,32,512]{2,1,0:T(8,128)S(1)} %get-tuple-element.23), channel_id=1, replica_groups=mesh['groups'=2,'row'=32,'col'=4,'rep'=2] {'col','rep'}, dimensions={0} | all-to-all | bytes 1048576 | tf_op jit(solution)/shard_map/all_to_all | solution.py:214
  222.6 1.3 back.5
  223.9 15.9 %all_to_all.74.pieces_ref = f32[8,32,256]{2,1,0:T(8,128)S(1)} all-to-all(f32[8,32,256]{2,1,0:T(8,128)S(1)} %get-tuple-element.25), channel_id=1, replica_groups={{0,8,16,24,32,40,48,56},{64,72,80,88,96,104,112,120},{128,136,144,152,1..., dimensions={0} | all-to-all | bytes 524288 | tf_op jit(solution)/shard_map/all_to_all | solution.py:214
  239.8 25.8 %all_to_all.75.pieces_ref = f32[4,32,256]{2,1,0:T(8,128)S(1)} all-to-all(f32[4,32,256]{2,1,0:T(8,128)S(1)} %sum.10), channel_id=1, replica_groups={{0,64,128,192},{8,72,136,200},{16,80,144,208},{24,88,152,216},{32,96,16..., dimensions={0} | all-to-all | bytes 262144 | tf_op jit(solution)/shard_map/all_to_all | solution.py:214
  265.7 20.1 %all_to_all.76.total_ref = f32[8,32,256]{2,1,0:T(8,128)S(1)} all-to-all(f32[8,32,256]{2,1,0:T(8,128)S(1)} %sum.11), channel_id=1, replica_groups={{64,72,80,88,32,40,48,56},{128,136,144,152,96,104,112,120},{192,200,208..., dimensions={0} | all-to-all | bytes 524288 | tf_op jit(solution)/shard_map/all_to_all | solution.py:214
  285.8 0.8 last.1
  286.6 13.9 %all_to_all.77.tables_ref = f32[8,8,128]{2,1,0:T(8,128)S(1)} all-to-all(f32[8,8,128]{2,1,0:T(8,128)S(1)} %get-tuple-element.30), channel_id=1, replica_groups=mesh['groups'=2,'row'=32,'col'=4,'rep'=2] {'col','rep'}, dimensions={0} | all-to-all | bytes 65536 | tf_op jit(solution)/shard_map/all_to_all | solution.py:214
  300.5 0.6 errors.1
  (7 shorter events, 0.1 us)
Async XLA Ops:
  0.6 2.2 copy-start
  2.8 49.8 %copy-start.2 = (f32[32,512]{1,0:T(8,128)S(1)}, f32[32,512]{1,0:T(8,128)}, u32[]{:S(2)}) copy-start(f32[32,512]{1,0:T(8,128)} %source_ref.5) | copy-start | bytes 196612
  4.0 123.1 %copy-start.1 = (f32[32,2048]{1,0:T(8,128)S(1)}, f32[32,2048]{1,0:T(8,128)}, u32[]{:S(2)}) copy-start(f32[32,2048]{1,0:T(8,128)} %target_ref.5) | copy-start | bytes 786436

commit v5 on v4

--- a/solution.py
+++ b/solution.py
@@ -230,12 +230,15 @@
         return [[device(row, core) for row in rows_of] for core in range(cores) for rows_of in members]
 
     half = NEAR // 2
-    starts = range(0, rows, NEAR)
-    sum_groups = groups_of([[start + i for i in range(NEAR)] for start in starts])
-    far_groups = groups_of([[start + i for start in starts] for i in range(NEAR)])
-    gather_groups = groups_of(
-        [[start + i + (NEAR if i < half else 0) for i in range(NEAR)] for start in starts]
-    )
+
+    def owner(group, piece):
+        moved = half // 2 if group % far >= far // 2 else 0
+        return group * NEAR + piece // half * half + (piece + moved) % half
+
+    pieces_of, groups = range(NEAR), range(far)
+    sum_groups = groups_of([[owner(g, m) for m in pieces_of] for g in groups])
+    far_groups = groups_of([[owner(g, m) for g in groups] for m in pieces_of])
+    gather_groups = groups_of([[owner(g + (m < half), m) for m in pieces_of] for g in groups])
 
     def total_over_rows(pieces):
         pieces = summed(exchange(pieces, lines, sum_groups), far)

time: 302 us -> 304 us (level)
  no operation moved by 1% of the time
where the time goes in v5:
time: 304 us; the launch traced here: 303 us
  blocking collectives  291 us (96%)
  Pallas kernels  9.37 us (3%)
    all_to_all x13, blocking collectives, exchange(): lax.all_to_all(pieces, axis, split_axis=0, concat_axis=0, tiled=True, axi...  291 us

profile of v5, /device:TPU:33, one launch (start us, length us, event | category | flops | bytes accessed | tf_op | source)
XLA Modules:
  0.0 303.1 jit_solution(967305344019894314)
XLA Ops:
  0.6 0.0 copy-start
  0.6 2.2 copy-done
  2.8 0.0 copy-start.2
  2.8 1.1 split.1
  4.0 0.0 copy-start.1
  4.0 48.6 %all_to_all.65.value_ref = f32[8,1,512]{2,1,0:T(1,128)S(1)} all-to-all(f32[8,1,512]{2,1,0:T(1,128)S(1)} %get-tuple-element.17), channel_id=1, replica_groups=mesh['groups'=2,'row'=32,'col'=4,'rep'=2] {'col','rep'}, dimensions={0} | all-to-all | bytes 32768 | tf_op jit(solution)/shard_map/all_to_all | solution.py:214
  52.6 0.0 copy-done.2
  52.6 1.3 back.3
  53.9 16.8 %all_to_all.66.pieces_ref = f32[8,32,256]{2,1,0:T(8,128)S(1)} all-to-all(f32[8,32,256]{2,1,0:T(8,128)S(1)} %get-tuple-element.19), channel_id=1, replica_groups={{0,8,16,24,32,40,48,56},{64,72,80,88,96,104,112,120},{144,152,128,136,1..., dimensions={0} | all-to-all | bytes 524288 | tf_op jit(solution)/shard_map/all_to_all | solution.py:214
  70.8 24.5 %all_to_all.67.pieces_ref = f32[4,32,256]{2,1,0:T(8,128)S(1)} all-to-all(f32[4,32,256]{2,1,0:T(8,128)S(1)} %sum.6), channel_id=1, replica_groups={{0,64,144,208},{8,72,152,216},{16,80,128,192},{24,88,136,200},{32,96,17..., dimensions={0} | all-to-all | bytes 262144 | tf_op jit(solution)/shard_map/all_to_all | solution.py:214
  95.3 29.3 %all_to_all.68.total_ref = f32[8,32,256]{2,1,0:T(8,128)S(1)} all-to-all(f32[8,32,256]{2,1,0:T(8,128)S(1)} %sum.7), channel_id=1, replica_groups={{64,72,80,88,32,40,48,56},{144,152,128,136,96,104,112,120},{208,216,192..., dimensions={0} | all-to-all | bytes 524288 | tf_op jit(solution)/shard_map/all_to_all | solution.py:214
  124.7 0.0 copy-done.1
  124.7 1.4 value.2
  126.1 11.7 %all_to_all.69.value_ref = f32[8,32,512]{2,1,0:T(8,128)S(1)} all-to-all(f32[8,32,512]{2,1,0:T(8,128)S(1)} %get-tuple-element.20), channel_id=1, replica_groups=mesh['groups'=2,'row'=32,'col'=4,'rep'=2] {'col','rep'}, dimensions={0} | all-to-all | bytes 1048576 | tf_op jit(solution)/shard_map/all_to_all | solution.py:214
  137.8 1.3 back.4
  139.1 17.9 %all_to_all.70.pieces_ref = f32[8,32,256]{2,1,0:T(8,128)S(1)} all-to-all(f32[8,32,256]{2,1,0:T(8,128)S(1)} %get-tuple-element.21), channel_id=1, replica_groups={{0,8,16,24,32,40,48,56},{64,72,80,88,96,104,112,120},{144,152,128,136,1..., dimensions={0} | all-to-all | bytes 524288 | tf_op jit(solution)/shard_map/all_to_all | solution.py:214
  157.0 24.2 %all_to_all.71.pieces_ref = f32[4,32,256]{2,1,0:T(8,128)S(1)} all-to-all(f32[4,32,256]{2,1,0:T(8,128)S(1)} %sum.8), channel_id=1, replica_groups={{0,64,144,208},{8,72,152,216},{16,80,128,192},{24,88,136,200},{32,96,17..., dimensions={0} | all-to-all | bytes 262144 | tf_op jit(solution)/shard_map/all_to_all | solution.py:214
  181.2 28.5 %all_to_all.72.total_ref = f32[8,32,256]{2,1,0:T(8,128)S(1)} all-to-all(f32[8,32,256]{2,1,0:T(8,128)S(1)} %sum.9), channel_id=1, replica_groups={{64,72,80,88,32,40,48,56},{144,152,128,136,96,104,112,120},{208,216,192..., dimensions={0} | all-to-all | bytes 524288 | tf_op jit(solution)/shard_map/all_to_all | solution.py:214
  209.7 1.4 value.3
  211.1 11.7 %all_to_all.73.value_ref = f32[8,32,512]{2,1,0:T(8,128)S(1)} all-to-all(f32[8,32,512]{2,1,0:T(8,128)S(1)} %get-tuple-element.23), channel_id=1, replica_groups=mesh['groups'=2,'row'=32,'col'=4,'rep'=2] {'col','rep'}, dimensions={0} | all-to-all | bytes 1048576 | tf_op jit(solution)/shard_map/all_to_all | solution.py:214
  222.8 1.3 back.5
  224.1 15.4 %all_to_all.74.pieces_ref = f32[8,32,256]{2,1,0:T(8,128)S(1)} all-to-all(f32[8,32,256]{2,1,0:T(8,128)S(1)} %get-tuple-element.25), channel_id=1, replica_groups={{0,8,16,24,32,40,48,56},{64,72,80,88,96,104,112,120},{144,152,128,136,1..., dimensions={0} | all-to-all | bytes 524288 | tf_op jit(solution)/shard_map/all_to_all | solution.py:214
  239.5 24.5 %all_to_all.75.pieces_ref = f32[4,32,256]{2,1,0:T(8,128)S(1)} all-to-all(f32[4,32,256]{2,1,0:T(8,128)S(1)} %sum.10), channel_id=1, replica_groups={{0,64,144,208},{8,72,152,216},{16,80,128,192},{24,88,136,200},{32,96,17..., dimensions={0} | all-to-all | bytes 262144 | tf_op jit(solution)/shard_map/all_to_all | solution.py:214
  264.1 30.6 %all_to_all.76.total_ref = f32[8,32,256]{2,1,0:T(8,128)S(1)} all-to-all(f32[8,32,256]{2,1,0:T(8,128)S(1)} %sum.11), channel_id=1, replica_groups={{64,72,80,88,32,40,48,56},{144,152,128,136,96,104,112,120},{208,216,192..., dimensions={0} | all-to-all | bytes 524288 | tf_op jit(solution)/shard_map/all_to_all | solution.py:214
  294.7 0.8 last.1
  295.4 7.0 %all_to_all.77.tables_ref = f32[8,8,128]{2,1,0:T(8,128)S(1)} all-to-all(f32[8,8,128]{2,1,0:T(8,128)S(1)} %get-tuple-element.30), channel_id=1, replica_groups=mesh['groups'=2,'row'=32,'col'=4,'rep'=2] {'col','rep'}, dimensions={0} | all-to-all | bytes 65536 | tf_op jit(solution)/shard_map/all_to_all | solution.py:214
  302.5 0.6 errors.1
  (7 shorter events, 0.1 us)
Async XLA Ops:
  0.6 2.2 copy-start
  2.8 49.8 %copy-start.2 = (f32[32,512]{1,0:T(8,128)S(1)}, f32[32,512]{1,0:T(8,128)}, u32[]{:S(2)}) copy-start(f32[32,512]{1,0:T(8,128)} %source_ref.5) | copy-start | bytes 196612
  4.0 120.7 %copy-start.1 = (f32[32,2048]{1,0:T(8,128)S(1)}, f32[32,2048]{1,0:T(8,128)}, u32[]{:S(2)}) copy-start(f32[32,2048]{1,0:T(8,128)} %target_ref.5) | copy-start | bytes 786436

commit v6 on v4

--- a/solution.py
+++ b/solution.py
@@ -9,6 +9,12 @@
 
 ITERS = 3
 NEAR = 8
+OWNERS = (
+    (2, 5, 4, 7, 1, 6, 0, 3),
+    (3, 1, 5, 6, 0, 7, 2, 4),
+    (4, 0, 2, 1, 6, 3, 5, 7),
+    (5, 4, 1, 7, 2, 0, 3, 6),
+)
 SPLIT_STEPS = 4
 LANES = 128
 SUBLANES = 8
@@ -229,18 +235,29 @@
     def groups_of(members):
         return [[device(row, core) for row in rows_of] for core in range(cores) for rows_of in members]
 
-    half = NEAR // 2
-    starts = range(0, rows, NEAR)
-    sum_groups = groups_of([[start + i for i in range(NEAR)] for start in starts])
-    far_groups = groups_of([[start + i for start in starts] for i in range(NEAR)])
-    gather_groups = groups_of(
-        [[start + i + (NEAR if i < half else 0) for i in range(NEAR)] for start in starts]
+    def apart(one, other):
+        return min((one - other) % rows, (other - one) % rows)
+
+    def longest(first, members):
+        entry = max(apart(k, first) for k in members)
+        return entry + max(apart(first, k) + apart(k, j) for k in members for j in members)
+
+    def first_chosen(members):
+        first = min(members, key=lambda row: longest(row, members))
+        return [first] + [row for row in members if row != first]
+
+    def owner(group, piece):
+        return group * NEAR + OWNERS[group][piece]
+
+    near_groups = groups_of([[owner(g, m) for m in range(NEAR)] for g in range(far)])
+    far_groups = groups_of(
+        [first_chosen([owner(g, m) for g in range(far)]) for m in range(NEAR)]
     )
 
     def total_over_rows(pieces):
-        pieces = summed(exchange(pieces, lines, sum_groups), far)
+        pieces = summed(exchange(pieces, lines, near_groups), far)
         pieces = summed(exchange(pieces, lines, far_groups), NEAR)
-        return exchange(pieces, lines, gather_groups)
+        return exchange(pieces, lines, near_groups)
 
     def local(kernel, source, target):
         split_kernel, sums = split(kernel, blocks)

time: 302 us -> 284 us (0.940)
  blocking collectives: 289 us -> 271 us
    all_to_all x13, blocking collectives: 289 us -> 271 us  [exchange(): lax.all_to_all(pieces, axis, split_axis=0, concat_axis=0, tiled=True, axi...]
where the time goes in v6:
time: 284 us; the launch traced here: 283 us
  blocking collectives  271 us (95%)
  Pallas kernels  9.38 us (3%)
    all_to_all x13, blocking collectives, exchange(): lax.all_to_all(pieces, axis, split_axis=0, concat_axis=0, tiled=True, axi...  271 us

profile of v6, /device:TPU:33, one launch (start us, length us, event | category | flops | bytes accessed | tf_op | source)
XLA Modules:
  0.0 282.9 jit_solution(2907880242245052574)
XLA Ops:
  0.6 0.0 copy-start
  0.6 2.2 copy-done
  2.8 0.0 copy-start.2
  2.8 1.1 split.1
  4.0 0.0 copy-start.1
  4.0 48.6 %all_to_all.65.value_ref = f32[8,1,512]{2,1,0:T(1,128)S(1)} all-to-all(f32[8,1,512]{2,1,0:T(1,128)S(1)} %get-tuple-element.17), channel_id=1, replica_groups=mesh['groups'=2,'row'=32,'col'=4,'rep'=2] {'col','rep'}, dimensions={0} | all-to-all | bytes 32768 | tf_op jit(solution)/shard_map/all_to_all | solution.py:220
  52.6 0.0 copy-done.2
  52.6 1.3 back.3
  53.9 19.6 %all_to_all.66.pieces_ref = f32[8,32,256]{2,1,0:T(8,128)S(1)} all-to-all(f32[8,32,256]{2,1,0:T(8,128)S(1)} %get-tuple-element.19), channel_id=1, replica_groups={{16,40,32,56,8,48,0,24},{88,72,104,112,64,120,80,96},{160,128,144,136,1..., dimensions={0} | all-to-all | bytes 524288 | tf_op jit(solution)/shard_map/all_to_all | solution.py:220
  73.6 24.1 %all_to_all.67.pieces_ref = f32[4,32,256]{2,1,0:T(8,128)S(1)} all-to-all(f32[4,32,256]{2,1,0:T(8,128)S(1)} %sum.6), channel_id=1, replica_groups={{16,88,160,232},{40,72,128,224},{104,32,144,200},{56,112,136,248},{8,64..., dimensions={0} | all-to-all | bytes 262144 | tf_op jit(solution)/shard_map/all_to_all | solution.py:220
  97.8 21.1 %all_to_all.68.total_ref = f32[8,32,256]{2,1,0:T(8,128)S(1)} all-to-all(f32[8,32,256]{2,1,0:T(8,128)S(1)} %sum.7), channel_id=1, replica_groups={{16,40,32,56,8,48,0,24},{88,72,104,112,64,120,80,96},{160,128,144,136,1..., dimensions={0} | all-to-all | bytes 524288 | tf_op jit(solution)/shard_map/all_to_all | solution.py:220
  118.9 0.0 copy-done.1
  118.9 1.4 value.2
  120.3 12.5 %all_to_all.69.value_ref = f32[8,32,512]{2,1,0:T(8,128)S(1)} all-to-all(f32[8,32,512]{2,1,0:T(8,128)S(1)} %get-tuple-element.20), channel_id=1, replica_groups=mesh['groups'=2,'row'=32,'col'=4,'rep'=2] {'col','rep'}, dimensions={0} | all-to-all | bytes 1048576 | tf_op jit(solution)/shard_map/all_to_all | solution.py:220
  132.8 1.3 back.4
  134.1 16.6 %all_to_all.70.pieces_ref = f32[8,32,256]{2,1,0:T(8,128)S(1)} all-to-all(f32[8,32,256]{2,1,0:T(8,128)S(1)} %get-tuple-element.21), channel_id=1, replica_groups={{16,40,32,56,8,48,0,24},{88,72,104,112,64,120,80,96},{160,128,144,136,1..., dimensions={0} | all-to-all | bytes 524288 | tf_op jit(solution)/shard_map/all_to_all | solution.py:220
  150.7 23.0 %all_to_all.71.pieces_ref = f32[4,32,256]{2,1,0:T(8,128)S(1)} all-to-all(f32[4,32,256]{2,1,0:T(8,128)S(1)} %sum.8), channel_id=1, replica_groups={{16,88,160,232},{40,72,128,224},{104,32,144,200},{56,112,136,248},{8,64..., dimensions={0} | all-to-all | bytes 262144 | tf_op jit(solution)/shard_map/all_to_all | solution.py:220
  173.7 14.0 %all_to_all.72.total_ref = f32[8,32,256]{2,1,0:T(8,128)S(1)} all-to-all(f32[8,32,256]{2,1,0:T(8,128)S(1)} %sum.9), channel_id=1, replica_groups={{16,40,32,56,8,48,0,24},{88,72,104,112,64,120,80,96},{160,128,144,136,1..., dimensions={0} | all-to-all | bytes 524288 | tf_op jit(solution)/shard_map/all_to_all | solution.py:220
  187.7 1.4 value.3
  189.1 21.1 %all_to_all.73.value_ref = f32[8,32,512]{2,1,0:T(8,128)S(1)} all-to-all(f32[8,32,512]{2,1,0:T(8,128)S(1)} %get-tuple-element.23), channel_id=1, replica_groups=mesh['groups'=2,'row'=32,'col'=4,'rep'=2] {'col','rep'}, dimensions={0} | all-to-all | bytes 1048576 | tf_op jit(solution)/shard_map/all_to_all | solution.py:220
  210.1 1.3 back.5
  211.5 17.0 %all_to_all.74.pieces_ref = f32[8,32,256]{2,1,0:T(8,128)S(1)} all-to-all(f32[8,32,256]{2,1,0:T(8,128)S(1)} %get-tuple-element.25), channel_id=1, replica_groups={{16,40,32,56,8,48,0,24},{88,72,104,112,64,120,80,96},{160,128,144,136,1..., dimensions={0} | all-to-all | bytes 524288 | tf_op jit(solution)/shard_map/all_to_all | solution.py:220
  228.4 22.7 %all_to_all.75.pieces_ref = f32[4,32,256]{2,1,0:T(8,128)S(1)} all-to-all(f32[4,32,256]{2,1,0:T(8,128)S(1)} %sum.10), channel_id=1, replica_groups={{16,88,160,232},{40,72,128,224},{104,32,144,200},{56,112,136,248},{8,64..., dimensions={0} | all-to-all | bytes 262144 | tf_op jit(solution)/shard_map/all_to_all | solution.py:220
  251.2 17.5 %all_to_all.76.total_ref = f32[8,32,256]{2,1,0:T(8,128)S(1)} all-to-all(f32[8,32,256]{2,1,0:T(8,128)S(1)} %sum.11), channel_id=1, replica_groups={{16,40,32,56,8,48,0,24},{88,72,104,112,64,120,80,96},{160,128,144,136,1..., dimensions={0} | all-to-all | bytes 524288 | tf_op jit(solution)/shard_map/all_to_all | solution.py:220
  268.7 0.8 last.1
  269.5 12.8 %all_to_all.77.tables_ref = f32[8,8,128]{2,1,0:T(8,128)S(1)} all-to-all(f32[8,8,128]{2,1,0:T(8,128)S(1)} %get-tuple-element.30), channel_id=1, replica_groups=mesh['groups'=2,'row'=32,'col'=4,'rep'=2] {'col','rep'}, dimensions={0} | all-to-all | bytes 65536 | tf_op jit(solution)/shard_map/all_to_all | solution.py:220
  282.4 0.6 errors.1
  (7 shorter events, 0.1 us)
Async XLA Ops:
  0.6 2.2 copy-start
  2.8 49.8 %copy-start.2 = (f32[32,512]{1,0:T(8,128)S(1)}, f32[32,512]{1,0:T(8,128)}, u32[]{:S(2)}) copy-start(f32[32,512]{1,0:T(8,128)} %source_ref.5) | copy-start | bytes 196612
  4.0 114.9 %copy-start.1 = (f32[32,2048]{1,0:T(8,128)S(1)}, f32[32,2048]{1,0:T(8,128)}, u32[]{:S(2)}) copy-start(f32[32,2048]{1,0:T(8,128)} %target_ref.5) | copy-start | bytes 786436

commit v7 on v6

--- a/solution.py
+++ b/solution.py
@@ -10,10 +10,14 @@
 ITERS = 3
 NEAR = 8
 OWNERS = (
-    (2, 5, 4, 7, 1, 6, 0, 3),
-    (3, 1, 5, 6, 0, 7, 2, 4),
-    (4, 0, 2, 1, 6, 3, 5, 7),
-    (5, 4, 1, 7, 2, 0, 3, 6),
+    (3, 7, 1, 4, 0, 5, 6, 2),
+    (3, 0, 2, 7, 1, 6, 5, 4),
+    (5, 3, 6, 2, 4, 0, 1, 7),
+    (5, 4, 7, 3, 6, 2, 1, 0),
+)
+FAR_FIRST = (
+    (3, 3, 3, 3, 3, 3, 3, 3),
+    (3, 3, 3, 3, 3, 2, 2, 2),
 )
 SPLIT_STEPS = 4
 LANES = 128
@@ -235,28 +239,20 @@
     def groups_of(members):
         return [[device(row, core) for row in rows_of] for core in range(cores) for rows_of in members]
 
-    def apart(one, other):
-        return min((one - other) % rows, (other - one) % rows)
-
-    def longest(first, members):
-        entry = max(apart(k, first) for k in members)
-        return entry + max(apart(first, k) + apart(k, j) for k in members for j in members)
-
-    def first_chosen(members):
-        first = min(members, key=lambda row: longest(row, members))
-        return [first] + [row for row in members if row != first]
-
     def owner(group, piece):
         return group * NEAR + OWNERS[group][piece]
 
     near_groups = groups_of([[owner(g, m) for m in range(NEAR)] for g in range(far)])
-    far_groups = groups_of(
-        [first_chosen([owner(g, m) for g in range(far)]) for m in range(NEAR)]
-    )
-
-    def total_over_rows(pieces):
+    far_groups = [
+        groups_of(
+            [[owner((first + i) % far, m) for i in range(far)] for m, first in enumerate(firsts)]
+        )
+        for firsts in FAR_FIRST
+    ]
+
+    def total_over_rows(pieces, step):
         pieces = summed(exchange(pieces, lines, near_groups), far)
-        pieces = summed(exchange(pieces, lines, far_groups), NEAR)
+        pieces = summed(exchange(pieces, lines, far_groups[min(step, 1)]), NEAR)
         return exchange(pieces, lines, near_groups)
 
     def local(kernel, source, target):
@@ -266,7 +262,7 @@
         terms = []
         for step in range(ITERS):
             left_scale, pieces = scale_left(values, source, split_kernel)
-            totals = total_over_rows(pieces)
+            totals = total_over_rows(pieces, step)
             if step < ITERS - 1:
                 right_scale, term, values = scale_right(
                     totals, target, right_scale, split_kernel, blocks

time: 284 us -> 281 us (0.989)
  blocking collectives: 271 us -> 267 us
    all_to_all x13, blocking collectives: 271 us -> 267 us  [exchange(): lax.all_to_all(pieces, axis, split_axis=0, concat_axis=0, tiled=True, axi...]
where the time goes in v7:
time: 281 us; the launch traced here: 279 us
  blocking collectives  267 us (95%)
  Pallas kernels  9.38 us (3%)
    all_to_all x13, blocking collectives, exchange(): lax.all_to_all(pieces, axis, split_axis=0, concat_axis=0, tiled=True, axi...  267 us

profile of v7, /device:TPU:33, one launch (start us, length us, event | category | flops | bytes accessed | tf_op | source)
XLA Modules:
  0.0 278.8 jit_solution(10575664277233798697)
XLA Ops:
  0.6 0.0 copy-start
  0.6 2.2 copy-done
  2.8 0.0 copy-start.2
  2.8 1.1 split.1
  4.0 0.0 copy-start.1
  4.0 48.6 %all_to_all.65.value_ref = f32[8,1,512]{2,1,0:T(1,128)S(1)} all-to-all(f32[8,1,512]{2,1,0:T(1,128)S(1)} %get-tuple-element.17), channel_id=1, replica_groups=mesh['groups'=2,'row'=32,'col'=4,'rep'=2] {'col','rep'}, dimensions={0} | all-to-all | bytes 32768 | tf_op jit(solution)/shard_map/all_to_all | solution.py:224
  52.6 0.0 copy-done.2
  52.6 1.3 back.3
  53.9 16.8 %all_to_all.66.pieces_ref = f32[8,32,256]{2,1,0:T(8,128)S(1)} all-to-all(f32[8,32,256]{2,1,0:T(8,128)S(1)} %get-tuple-element.19), channel_id=1, replica_groups={{24,56,8,32,0,40,48,16},{88,64,80,120,72,112,104,96},{168,152,176,144,1..., dimensions={0} | all-to-all | bytes 524288 | tf_op jit(solution)/shard_map/all_to_all | solution.py:224
  70.8 22.2 %all_to_all.67.pieces_ref = f32[4,32,256]{2,1,0:T(8,128)S(1)} all-to-all(f32[4,32,256]{2,1,0:T(8,128)S(1)} %sum.6), channel_id=1, replica_groups={{232,24,88,168},{224,56,64,152},{248,8,80,176},{216,32,120,144},{240,0,..., dimensions={0} | all-to-all | bytes 262144 | tf_op jit(solution)/shard_map/all_to_all | solution.py:224
  93.1 18.9 %all_to_all.68.total_ref = f32[8,32,256]{2,1,0:T(8,128)S(1)} all-to-all(f32[8,32,256]{2,1,0:T(8,128)S(1)} %sum.7), channel_id=1, replica_groups={{24,56,8,32,0,40,48,16},{88,64,80,120,72,112,104,96},{168,152,176,144,1..., dimensions={0} | all-to-all | bytes 524288 | tf_op jit(solution)/shard_map/all_to_all | solution.py:224
  111.9 0.0 copy-done.1
  112.0 1.4 value.2
  113.4 15.3 %all_to_all.69.value_ref = f32[8,32,512]{2,1,0:T(8,128)S(1)} all-to-all(f32[8,32,512]{2,1,0:T(8,128)S(1)} %get-tuple-element.20), channel_id=1, replica_groups=mesh['groups'=2,'row'=32,'col'=4,'rep'=2] {'col','rep'}, dimensions={0} | all-to-all | bytes 1048576 | tf_op jit(solution)/shard_map/all_to_all | solution.py:224
  128.6 1.3 back.4
  129.9 17.4 %all_to_all.70.pieces_ref = f32[8,32,256]{2,1,0:T(8,128)S(1)} all-to-all(f32[8,32,256]{2,1,0:T(8,128)S(1)} %get-tuple-element.21), channel_id=1, replica_groups={{24,56,8,32,0,40,48,16},{88,64,80,120,72,112,104,96},{168,152,176,144,1..., dimensions={0} | all-to-all | bytes 524288 | tf_op jit(solution)/shard_map/all_to_all | solution.py:224
  147.4 30.4 %all_to_all.71.pieces_ref = f32[4,32,256]{2,1,0:T(8,128)S(1)} all-to-all(f32[4,32,256]{2,1,0:T(8,128)S(1)} %sum.8), channel_id=1, replica_groups={{232,24,88,168},{224,56,64,152},{248,8,80,176},{216,32,120,144},{240,0,..., dimensions={0} | all-to-all | bytes 262144 | tf_op jit(solution)/shard_map/all_to_all | solution.py:224
  177.8 12.2 %all_to_all.72.total_ref = f32[8,32,256]{2,1,0:T(8,128)S(1)} all-to-all(f32[8,32,256]{2,1,0:T(8,128)S(1)} %sum.9), channel_id=1, replica_groups={{24,56,8,32,0,40,48,16},{88,64,80,120,72,112,104,96},{168,152,176,144,1..., dimensions={0} | all-to-all | bytes 524288 | tf_op jit(solution)/shard_map/all_to_all | solution.py:224
  190.0 1.4 value.3
  191.4 14.2 %all_to_all.73.value_ref = f32[8,32,512]{2,1,0:T(8,128)S(1)} all-to-all(f32[8,32,512]{2,1,0:T(8,128)S(1)} %get-tuple-element.23), channel_id=1, replica_groups=mesh['groups'=2,'row'=32,'col'=4,'rep'=2] {'col','rep'}, dimensions={0} | all-to-all | bytes 1048576 | tf_op jit(solution)/shard_map/all_to_all | solution.py:224
  205.7 1.3 back.5
  207.0 18.1 %all_to_all.74.pieces_ref = f32[8,32,256]{2,1,0:T(8,128)S(1)} all-to-all(f32[8,32,256]{2,1,0:T(8,128)S(1)} %get-tuple-element.25), channel_id=1, replica_groups={{24,56,8,32,0,40,48,16},{88,64,80,120,72,112,104,96},{168,152,176,144,1..., dimensions={0} | all-to-all | bytes 524288 | tf_op jit(solution)/shard_map/all_to_all | solution.py:224
  225.1 30.8 %all_to_all.75.pieces_ref = f32[4,32,256]{2,1,0:T(8,128)S(1)} all-to-all(f32[4,32,256]{2,1,0:T(8,128)S(1)} %sum.10), channel_id=1, replica_groups={{232,24,88,168},{224,56,64,152},{248,8,80,176},{216,32,120,144},{240,0,..., dimensions={0} | all-to-all | bytes 262144 | tf_op jit(solution)/shard_map/all_to_all | solution.py:224
  255.9 12.2 %all_to_all.76.total_ref = f32[8,32,256]{2,1,0:T(8,128)S(1)} all-to-all(f32[8,32,256]{2,1,0:T(8,128)S(1)} %sum.11), channel_id=1, replica_groups={{24,56,8,32,0,40,48,16},{88,64,80,120,72,112,104,96},{168,152,176,144,1..., dimensions={0} | all-to-all | bytes 524288 | tf_op jit(solution)/shard_map/all_to_all | solution.py:224
  268.1 0.8 last.1
  268.9 9.3 %all_to_all.77.tables_ref = f32[8,8,128]{2,1,0:T(8,128)S(1)} all-to-all(f32[8,8,128]{2,1,0:T(8,128)S(1)} %get-tuple-element.30), channel_id=1, replica_groups=mesh['groups'=2,'row'=32,'col'=4,'rep'=2] {'col','rep'}, dimensions={0} | all-to-all | bytes 65536 | tf_op jit(solution)/shard_map/all_to_all | solution.py:224
  278.2 0.6 errors.1
  (7 shorter events, 0.1 us)
Async XLA Ops:
  0.6 2.2 copy-start
  2.8 49.8 %copy-start.2 = (f32[32,512]{1,0:T(8,128)S(1)}, f32[32,512]{1,0:T(8,128)}, u32[]{:S(2)}) copy-start(f32[32,512]{1,0:T(8,128)} %source_ref.5) | copy-start | bytes 196612
  4.0 108.0 %copy-start.1 = (f32[32,2048]{1,0:T(8,128)S(1)}, f32[32,2048]{1,0:T(8,128)}, u32[]{:S(2)}) copy-start(f32[32,2048]{1,0:T(8,128)} %target_ref.5) | copy-start | bytes 786436

commit v8 on v7

--- a/solution.py
+++ b/solution.py
@@ -232,6 +232,7 @@
     block = ("col", "rep")
     blocks = mesh.shape["col"] * cores
     lines = ("row", "rep")
+    block_group = [[cores - 1] + [i for i in range(blocks) if i != cores - 1]]
 
     def device(row, core):
         return (row + core * NEAR // cores) % rows * cores + core
@@ -257,7 +258,7 @@
 
     def local(kernel, source, target):
         split_kernel, sums = split(kernel, blocks)
-        values = exchange(sums, block)
+        values = exchange(sums, block, block_group)
         right_scale = jnp.ones(target.shape, f32)
         terms = []
         for step in range(ITERS):
@@ -267,11 +268,11 @@
                 right_scale, term, values = scale_right(
                     totals, target, right_scale, split_kernel, blocks
                 )
-                values = exchange(values, block)
+                values = exchange(values, block, block_group)
                 terms.append(term)
         right_scale, tables = last_right(totals, target, right_scale, terms, blocks)
         count = float(blocks * target.shape[1])
-        errors = mean_errors(exchange(tables, block), target.shape[0], count)
+        errors = mean_errors(exchange(tables, block, block_group), target.shape[0], count)
         return left_scale, right_scale, errors
 
     return jax.shard_map(

time: 281 us -> 279 us (level)
  no operation moved by 1% of the time
where the time goes in v8:
time: 279 us; the launch traced here: 277 us
  blocking collectives  265 us (95%)
  Pallas kernels  9.37 us (3%)
    all_to_all x13, blocking collectives, exchange(): lax.all_to_all(pieces, axis, split_axis=0, concat_axis=0, tiled=True, axi...  265 us

profile of v8, /device:TPU:33, one launch (start us, length us, event | category | flops | bytes accessed | tf_op | source)
XLA Modules:
  0.0 277.5 jit_solution(2654838342270569679)
XLA Ops:
  0.6 0.0 copy-start
  0.6 2.2 copy-done
  2.8 0.0 copy-start.2
  2.8 1.1 split.1
  4.0 0.0 copy-start.1
  4.0 47.7 %all_to_all.65.value_ref = f32[8,1,512]{2,1,0:T(1,128)S(1)} all-to-all(f32[8,1,512]{2,1,0:T(1,128)S(1)} %get-tuple-element.17), channel_id=1, replica_groups={{1,0,2,3,4,5,6,7},{9,8,10,11,12,13,14,15},{17,16,18,19,20,21,22,23},{25..., dimensions={0} | all-to-all | bytes 32768 | tf_op jit(solution)/shard_map/all_to_all | solution.py:224
  51.7 0.0 copy-done.2
  51.7 1.3 back.3
  53.0 18.5 %all_to_all.66.pieces_ref = f32[8,32,256]{2,1,0:T(8,128)S(1)} all-to-all(f32[8,32,256]{2,1,0:T(8,128)S(1)} %get-tuple-element.19), channel_id=1, replica_groups={{24,56,8,32,0,40,48,16},{88,64,80,120,72,112,104,96},{168,152,176,144,1..., dimensions={0} | all-to-all | bytes 524288 | tf_op jit(solution)/shard_map/all_to_all | solution.py:224
  71.5 27.9 %all_to_all.67.pieces_ref = f32[4,32,256]{2,1,0:T(8,128)S(1)} all-to-all(f32[4,32,256]{2,1,0:T(8,128)S(1)} %sum.6), channel_id=1, replica_groups={{232,24,88,168},{224,56,64,152},{248,8,80,176},{216,32,120,144},{240,0,..., dimensions={0} | all-to-all | bytes 262144 | tf_op jit(solution)/shard_map/all_to_all | solution.py:224
  99.4 12.2 %all_to_all.68.total_ref = f32[8,32,256]{2,1,0:T(8,128)S(1)} all-to-all(f32[8,32,256]{2,1,0:T(8,128)S(1)} %sum.7), channel_id=1, replica_groups={{24,56,8,32,0,40,48,16},{88,64,80,120,72,112,104,96},{168,152,176,144,1..., dimensions={0} | all-to-all | bytes 524288 | tf_op jit(solution)/shard_map/all_to_all | solution.py:224
  111.6 0.0 copy-done.1
  111.7 1.4 value.2
  113.0 14.0 %all_to_all.69.value_ref = f32[8,32,512]{2,1,0:T(8,128)S(1)} all-to-all(f32[8,32,512]{2,1,0:T(8,128)S(1)} %get-tuple-element.20), channel_id=1, replica_groups={{1,0,2,3,4,5,6,7},{9,8,10,11,12,13,14,15},{17,16,18,19,20,21,22,23},{25..., dimensions={0} | all-to-all | bytes 1048576 | tf_op jit(solution)/shard_map/all_to_all | solution.py:224
  127.1 1.3 back.4
  128.4 19.4 %all_to_all.70.pieces_ref = f32[8,32,256]{2,1,0:T(8,128)S(1)} all-to-all(f32[8,32,256]{2,1,0:T(8,128)S(1)} %get-tuple-element.21), channel_id=1, replica_groups={{24,56,8,32,0,40,48,16},{88,64,80,120,72,112,104,96},{168,152,176,144,1..., dimensions={0} | all-to-all | bytes 524288 | tf_op jit(solution)/shard_map/all_to_all | solution.py:224
  147.8 29.6 %all_to_all.71.pieces_ref = f32[4,32,256]{2,1,0:T(8,128)S(1)} all-to-all(f32[4,32,256]{2,1,0:T(8,128)S(1)} %sum.8), channel_id=1, replica_groups={{232,24,88,168},{224,56,64,152},{248,8,80,176},{216,32,120,144},{240,0,..., dimensions={0} | all-to-all | bytes 262144 | tf_op jit(solution)/shard_map/all_to_all | solution.py:224
  177.5 13.3 %all_to_all.72.total_ref = f32[8,32,256]{2,1,0:T(8,128)S(1)} all-to-all(f32[8,32,256]{2,1,0:T(8,128)S(1)} %sum.9), channel_id=1, replica_groups={{24,56,8,32,0,40,48,16},{88,64,80,120,72,112,104,96},{168,152,176,144,1..., dimensions={0} | all-to-all | bytes 524288 | tf_op jit(solution)/shard_map/all_to_all | solution.py:224
  190.8 1.4 value.3
  192.2 13.4 %all_to_all.73.value_ref = f32[8,32,512]{2,1,0:T(8,128)S(1)} all-to-all(f32[8,32,512]{2,1,0:T(8,128)S(1)} %get-tuple-element.23), channel_id=1, replica_groups={{1,0,2,3,4,5,6,7},{9,8,10,11,12,13,14,15},{17,16,18,19,20,21,22,23},{25..., dimensions={0} | all-to-all | bytes 1048576 | tf_op jit(solution)/shard_map/all_to_all | solution.py:224
  205.6 1.3 back.5
  206.9 18.3 %all_to_all.74.pieces_ref = f32[8,32,256]{2,1,0:T(8,128)S(1)} all-to-all(f32[8,32,256]{2,1,0:T(8,128)S(1)} %get-tuple-element.25), channel_id=1, replica_groups={{24,56,8,32,0,40,48,16},{88,64,80,120,72,112,104,96},{168,152,176,144,1..., dimensions={0} | all-to-all | bytes 524288 | tf_op jit(solution)/shard_map/all_to_all | solution.py:224
  225.2 29.5 %all_to_all.75.pieces_ref = f32[4,32,256]{2,1,0:T(8,128)S(1)} all-to-all(f32[4,32,256]{2,1,0:T(8,128)S(1)} %sum.10), channel_id=1, replica_groups={{232,24,88,168},{224,56,64,152},{248,8,80,176},{216,32,120,144},{240,0,..., dimensions={0} | all-to-all | bytes 262144 | tf_op jit(solution)/shard_map/all_to_all | solution.py:224
  254.7 13.3 %all_to_all.76.total_ref = f32[8,32,256]{2,1,0:T(8,128)S(1)} all-to-all(f32[8,32,256]{2,1,0:T(8,128)S(1)} %sum.11), channel_id=1, replica_groups={{24,56,8,32,0,40,48,16},{88,64,80,120,72,112,104,96},{168,152,176,144,1..., dimensions={0} | all-to-all | bytes 524288 | tf_op jit(solution)/shard_map/all_to_all | solution.py:224
  268.0 0.8 last.1
  268.8 8.1 %all_to_all.77.tables_ref = f32[8,8,128]{2,1,0:T(8,128)S(1)} all-to-all(f32[8,8,128]{2,1,0:T(8,128)S(1)} %get-tuple-element.30), channel_id=1, replica_groups={{1,0,2,3,4,5,6,7},{9,8,10,11,12,13,14,15},{17,16,18,19,20,21,22,23},{25..., dimensions={0} | all-to-all | bytes 65536 | tf_op jit(solution)/shard_map/all_to_all | solution.py:224
  276.9 0.6 errors.1
  (7 shorter events, 0.1 us)
Async XLA Ops:
  0.6 2.2 copy-start
  2.8 48.9 %copy-start.2 = (f32[32,512]{1,0:T(8,128)S(1)}, f32[32,512]{1,0:T(8,128)}, u32[]{:S(2)}) copy-start(f32[32,512]{1,0:T(8,128)} %source_ref.5) | copy-start | bytes 196612
  4.0 107.7 %copy-start.1 = (f32[32,2048]{1,0:T(8,128)S(1)}, f32[32,2048]{1,0:T(8,128)}, u32[]{:S(2)}) copy-start(f32[32,2048]{1,0:T(8,128)} %target_ref.5) | copy-start | bytes 786436
